TPU v7x, 768 devices: a whole 4x8x12 slice. The times are simulated.
768 devices in a mesh: tm: 8 (over x, core), space: 96 (over y, z).
Axes of the slice: x: 4, y: 8, z: 12, core: 2. Of those that a mesh axis runs over, the one named last changes fastest.
Arguments:
- start_value: float32 [8, 96, 512, 256], P('tm', 'space'), may hold values from -6 to 6
- old_nodes: float32 [8, 3, 96, 512, 256], P('tm', None, 'space'), may hold values from -6 to 6
- diffusivity: float32 [96, 512, 256], P('space'), may hold values from 0.2 to 2
Outputs:
- fine_nodes: float32 [8, 3, 96, 512, 256], P('tm', None, 'space')
- next_start: float32 [8, 96, 512, 256], P('tm', 'space')
- next_coarse: float32 [8, 96, 512, 256], P('tm', 'space')
All inputs are finite; a program needn't handle non-finite values.
Results may differ from a plain program's by a relative error of at most 0.0001.
Values sent between devices are 32-bit elements; how exact they have to be, the bound alone decides.
A program may use at most 64 MiB of HBM per device.

v0:
```python
import math

import jax
import jax.numpy as jnp
from jax import lax
from jax.sharding import Mesh
from jax.sharding import PartitionSpec as P

CG_ITERS = 2
SPACE = ("space_0", "space_1")


STEP = 2.0
ROOT_SIX = math.sqrt(6.0)
NODE_TIMES = [(4.0 - ROOT_SIX) / 10.0, (4.0 + ROOT_SIX) / 10.0, 1.0]
COLLOC = [
    [
        (88.0 - 7.0 * ROOT_SIX) / 360.0,
        (296.0 - 169.0 * ROOT_SIX) / 1800.0,
        (-2.0 + 3.0 * ROOT_SIX) / 225.0,
    ],
    [
        (296.0 + 169.0 * ROOT_SIX) / 1800.0,
        (88.0 + 7.0 * ROOT_SIX) / 360.0,
        (-2.0 - 3.0 * ROOT_SIX) / 225.0,
    ],
    [(16.0 - ROOT_SIX) / 36.0, (16.0 + ROOT_SIX) / 36.0, 1.0 / 9.0],
]


def one_axis_at_a_time(value, axes):
    for axis in axes:
        value = lax.psum(value, axis)
    return value


def padded_2(value, sides, width):
    for axis, dim in sides:
        devices, length = (lax.axis_size(axis), value.shape[dim])
        up = [(i, (i + 1) % devices) for i in range(devices - 1)]
        down = [(j, i) for i, j in up]
        last = lax.slice_in_dim(value, length - width, length, axis=dim)
        leading = lax.slice_in_dim(value, 0, width, axis=dim)
        before = lax.ppermute(last, axis, up)
        after = lax.ppermute(leading, axis, down)
        value = jnp.concatenate([before, value, after], axis=dim)
    return value


def from_behind(block, axis, distance):
    devices = range(lax.axis_size(axis))
    route = [(i - distance, i) for i in devices if i - distance in devices]
    return lax.ppermute(block, axis, route)


def sweep_weight(row, column):
    below = COLLOC[row - 1][column] if row > 0 else 0.0
    return COLLOC[row][column] - below


def node_width(row):
    below = NODE_TIMES[row - 1] if row > 0 else 0.0
    return NODE_TIMES[row] - below


def neighbour(field, dim, forward):
    length = field.shape[dim]
    edge = jnp.zeros_like(lax.slice_in_dim(field, 0, 1, axis=dim))
    if forward:
        return jnp.concatenate([lax.slice_in_dim(field, 1, length, axis=dim), edge], axis=dim)
    return jnp.concatenate([edge, lax.slice_in_dim(field, 0, length - 1, axis=dim)], axis=dim)


def combine(weights, images):
    summed = weights[0] * images[0]
    for column in range(1, 3):
        summed = summed + weights[column] * images[column]
    return summed


def inner(left, right):
    return jnp.sum(left * right, axis=(1, 2, 3))


def widen(values):
    return values[:, None, None, None]


def paired(residual, image):
    return (
        one_axis_at_a_time(inner(residual, residual), SPACE),
        one_axis_at_a_time(inner(residual, image), SPACE),
    )


def solve(guess, residual, widths, heat):
    width_grid = widen(widths)
    iterate = guess
    image = residual - width_grid * heat(residual)
    norm_now, product_sum = paired(residual, image)
    step_size = norm_now / product_sum
    direction = residual
    along_image = image
    for sweep in range(CG_ITERS):
        iterate = iterate + widen(step_size) * direction
        if sweep + 1 < CG_ITERS:
            residual = residual - widen(step_size) * along_image
            image = residual - width_grid * heat(residual)
            norm_next, product_sum = paired(residual, image)
            momentum = norm_next / norm_now
            step_size = norm_next / (product_sum - momentum * norm_next / step_size)
            direction = residual + widen(momentum) * direction
            along_image = image + widen(momentum) * along_image
            norm_now = norm_next
    return iterate


def on_device(start_value, old_nodes, diffusivity):
    padded_kappa = padded_2(diffusivity, ((SPACE, 0),), 1)
    kappa_after = padded_kappa[2:]
    kappa_before = padded_kappa[:-2]

    def heat(stacked):
        padded = padded_2(stacked, ((SPACE, 1),), 1)
        face_one = 0.5 * (diffusivity + kappa_after)
        face_two = 0.5 * (diffusivity + kappa_before)
        face_three = 0.5 * (diffusivity + neighbour(diffusivity, 1, True))
        face_four = 0.5 * (diffusivity + neighbour(diffusivity, 1, False))
        face_five = 0.5 * (diffusivity + neighbour(diffusivity, 2, True))
        face_six = 0.5 * (diffusivity + neighbour(diffusivity, 2, False))
        total = face_one + face_two + face_three + face_four + face_five + face_six
        result = face_one * padded[:, 2:] + face_two * padded[:, :-2]
        result = (
            result
            + face_three * neighbour(stacked, 2, True)
            + face_four * neighbour(stacked, 2, False)
        )
        result = (
            result
            + face_five * neighbour(stacked, 3, True)
            + face_six * neighbour(stacked, 3, False)
        )
        return result - total * stacked

    previous_nodes = old_nodes[0]
    begin = start_value[0]
    images = heat(previous_nodes)

    def fine_residual(row, previous):
        weights = [sweep_weight(row, column) for column in range(3)]
        return previous - previous_nodes[row] + STEP * combine(weights, images)

    coarse_res = begin - previous_nodes[2] + STEP * combine(COLLOC[2], images)
    first_res = fine_residual(0, begin)
    together = solve(
        jnp.stack([previous_nodes[0], previous_nodes[2]]),
        jnp.stack([first_res, coarse_res]),
        jnp.array([STEP * node_width(0), STEP], jnp.float32),
        heat,
    )
    fresh = [together[0]]
    coarse_end = together[1]
    for row in range(1, 3):
        residual = fine_residual(row, fresh[row - 1])
        result = solve(
            previous_nodes[row : row + 1],
            residual[None],
            jnp.array([STEP * node_width(row)], jnp.float32),
            heat,
        )
        fresh.append(result[0])
    moved = from_behind(jnp.stack([fresh[2], coarse_end]), "tm", 1)
    first_slice = lax.axis_index("tm") == 0
    next_start = jnp.where(first_slice, begin, moved[0])[None]
    next_coarse = jnp.where(first_slice, begin, moved[1])[None]
    return (jnp.stack(fresh)[None], next_start, next_coarse)


def solution(mesh):
    split = Mesh(mesh.devices.reshape(mesh.shape["tm"], 8, 12), ("tm", "space_0", "space_1"))
    in_specs = (P("tm", SPACE, None, None), P("tm", None, SPACE, None, None), P(SPACE, None, None))
    out_specs = (
        P("tm", None, SPACE, None, None),
        P("tm", SPACE, None, None),
        P("tm", SPACE, None, None),
    )
    return jax.shard_map(
        on_device, mesh=split, in_specs=in_specs, out_specs=out_specs, check_vma=False
    )
```

profile of v0, /device:TPU:1, one launch (start us, length us, event | category | flops | bytes accessed | tf_op | source)
XLA Modules:
  0.0 474.9 jit_solution(12278737998373692713)
XLA Ops:
  0.6 1.4 collective-permute-start.1
  2.1 5.5 %collective-permute-start.3 = (f32[3,1,512,256]{3,2,1,0:T(8,128)}, f32[3,1,512,256]{3,2,1,0:T(8,128)S(1)}, u32[]{:S(2)}, u32[]{:S(2)}) collective-permute-start(f32[3,1,512,256]{3,2,1,0:T(8,128)} %bitcast.208), channel_id=1, source_target_pairs={{0,1},{1,2},{2,3},{3,4},{4,5},{5,6},{6,7},{7,8},{8,9},{9,10},{10,1... | collective-permute-start | bytes 4718600 | tf_op jit(solution)/shard_map/ppermute | solution.py:44
  7.6 1.3 collective-permute-start
  8.9 4.6 collective-permute-start.2
  13.5 1.4 fusion.57
  16.6 25.9 %collective-permute-done = f32[1,512,256]{2,1,0:T(8,128)S(1)} collective-permute-done((f32[1,512,256]{2,1,0:T(8,128)}, f32[1,512,256]{2,1,0:T(8,128)S(1)}, u32[]{:S(2)}, u32[]{:S(2)}) %collective-permute-start) | collective-permute-done | bytes 524320 | tf_op jit(solution)/shard_map/ppermute | solution.py:45
  44.0 1.4 multiply_subtract_fusion
  46.6 1.3 collective-permute-start.4
  47.9 12.3 %collective-permute-start.5 = (f32[2,1,512,256]{3,2,1,0:T(8,128)S(1)}, f32[2,1,512,256]{3,2,1,0:T(8,128)S(1)}, u32[]{:S(2)}, u32[]{:S(2)}) collective-permute-start(f32[2,1,512,256]{3,2,1,0:T(8,128)S(1)} %pad_maximum_fusion), channel_id=1, source_target_pairs={{0,1},{1,2},{2,3},{3,4},{4,5},{5,6},{6,7},{7,8},{8,9},{9,10},{10,1... | collective-permute-start | bytes 3145736 | tf_op jit(solution)/shard_map/ppermute | solution.py:44
  60.8 18.5 %collective-permute-done.4 = f32[2,1,512,256]{3,2,1,0:T(8,128)S(1)} collective-permute-done((f32[2,1,512,256]{3,2,1,0:T(8,128)S(1)}, f32[2,1,512,256]{3,2,1,0:T(8,128)S(1)}, u32[]{:S(2)}, u32[]{:S(2)}) %collective-permute-start.4) | collective-permute-done | bytes 1048608 | tf_op jit(solution)/shard_map/ppermute | solution.py:45
  80.2 2.2 multiply_reduce_fusion.1
  82.4 32.8 %all-reduce.43 = (f32[2]{0:T(128)S(1)}, f32[2]{0:T(128)S(1)}) all-reduce(f32[2]{0:T(128)S(1)} %get-tuple-element.6, f32[2]{0:T(128)S(1)} %get-tuple-element.5), channel_id=1, replica_groups=mesh['tm'=8,'space_0'=8,'space_1'=12] {'space_0'}, use_global_device_ids=true, to_apply=%region_1.0 | all-reduce | flops 4 | bytes 32 | tf_op jit(solution)/shard_map/psum | solution.py:33
  115.2 15.4 %all-reduce.37 = (f32[2]{0:T(128)S(1)}, f32[2]{0:T(128)S(1)}) all-reduce(f32[2]{0:T(128)S(1)} %get-tuple-element.37, f32[2]{0:T(128)S(1)} %get-tuple-element.38), channel_id=1, replica_groups=mesh['tm'=8,'space_0'=8,'space_1'=12] {'space_1'}, use_global_device_ids=true, to_apply=%region_2.0 | all-reduce | flops 4 | bytes 32 | tf_op jit(solution)/shard_map/psum | solution.py:33
  130.6 2.0 multiply_subtract_fusion.1
  132.5 1.3 collective-permute-start.6
  133.8 4.4 collective-permute-start.7
  139.8 8.6 %collective-permute-done.6 = f32[2,1,512,256]{3,2,1,0:T(8,128)S(1)} collective-permute-done((f32[2,1,512,256]{3,2,1,0:T(8,128)S(1)}, f32[2,1,512,256]{3,2,1,0:T(8,128)S(1)}, u32[]{:S(2)}, u32[]{:S(2)}) %collective-permute-start.6) | collective-permute-done | bytes 1048608 | tf_op jit(solution)/shard_map/ppermute | solution.py:45
  148.4 1.5 collective-permute-done.7
  150.0 1.3 fusion
  151.3 17.9 %all-reduce.42 = (f32[2]{0:T(128)S(1)}, f32[2]{0:T(128)S(1)}) all-reduce(f32[2]{0:T(128)S(1)} %get-tuple-element.4, f32[2]{0:T(128)S(1)} %get-tuple-element.3), channel_id=1, replica_groups=mesh['tm'=8,'space_0'=8,'space_1'=12] {'space_0'}, use_global_device_ids=true, to_apply=%region_7.0 | all-reduce | flops 4 | bytes 32 | tf_op jit(solution)/shard_map/psum | solution.py:33
  169.1 15.6 %all-reduce.36 = (f32[2]{0:T(128)S(1)}, f32[2]{0:T(128)S(1)}) all-reduce(f32[2]{0:T(128)S(1)} %get-tuple-element.35, f32[2]{0:T(128)S(1)} %get-tuple-element.36), channel_id=1, replica_groups=mesh['tm'=8,'space_0'=8,'space_1'=12] {'space_1'}, use_global_device_ids=true, to_apply=%region_8.0 | all-reduce | flops 4 | bytes 32 | tf_op jit(solution)/shard_map/psum | solution.py:33
  184.8 2.6 fusion.5
  189.9 4.0 collective-permute-start.9
  194.2 4.4 collective-permute-done.8
  198.6 1.5 collective-permute-done.9
  200.1 2.0 multiply_reduce_fusion.7
  202.1 17.8 %all-reduce.41 = (f32[1]{0:T(128)}, f32[1]{0:T(128)}) all-reduce(f32[1]{0:T(128)} %bitcast.11, f32[1]{0:T(128)} %bitcast.19), channel_id=1, replica_groups=mesh['tm'=8,'space_0'=8,'space_1'=12] {'space_0'}, use_global_device_ids=true, to_apply=%region_13.0 | all-reduce | flops 2 | bytes 16 | tf_op jit(solution)/shard_map/psum | solution.py:33
  219.9 16.2 %all-reduce.35 = (f32[1]{0:T(128)}, f32[1]{0:T(128)}) all-reduce(f32[1]{0:T(128)} %get-tuple-element.33, f32[1]{0:T(128)} %get-tuple-element.34), channel_id=1, replica_groups=mesh['tm'=8,'space_0'=8,'space_1'=12] {'space_1'}, use_global_device_ids=true, to_apply=%region_14.0 | all-reduce | flops 2 | bytes 16 | tf_op jit(solution)/shard_map/psum | solution.py:33
  240.0 4.2 collective-permute-start.11
  244.5 4.1 collective-permute-done.10
  248.6 1.5 collective-permute-done.11
  251.3 18.1 %all-reduce.40 = (f32[1]{0:T(128)}, f32[1]{0:T(128)}) all-reduce(f32[1]{0:T(128)} %bitcast.21, f32[1]{0:T(128)} %bitcast.22), channel_id=1, replica_groups=mesh['tm'=8,'space_0'=8,'space_1'=12] {'space_0'}, use_global_device_ids=true, to_apply=%region_19.0 | all-reduce | flops 2 | bytes 16 | tf_op jit(solution)/shard_map/psum | solution.py:33
  269.4 16.4 %all-reduce.34 = (f32[1]{0:T(128)}, f32[1]{0:T(128)}) all-reduce(f32[1]{0:T(128)} %get-tuple-element.31, f32[1]{0:T(128)} %get-tuple-element.32), channel_id=1, replica_groups=mesh['tm'=8,'space_0'=8,'space_1'=12] {'space_1'}, use_global_device_ids=true, to_apply=%region_20.0 | all-reduce | flops 2 | bytes 16 | tf_op jit(solution)/shard_map/psum | solution.py:33
  290.2 2.7 multiply_add_fusion.2
  294.2 4.3 collective-permute-start.13
  298.8 4.3 collective-permute-done.12
  303.0 1.5 collective-permute-done.13
  304.5 2.0 multiply_reduce_fusion.4
  306.5 17.5 %all-reduce.39 = (f32[1]{0:T(128)}, f32[1]{0:T(128)}) all-reduce(f32[1]{0:T(128)} %bitcast.25, f32[1]{0:T(128)} %bitcast.26), channel_id=1, replica_groups=mesh['tm'=8,'space_0'=8,'space_1'=12] {'space_0'}, use_global_device_ids=true, to_apply=%region_25.0 | all-reduce | flops 2 | bytes 16 | tf_op jit(solution)/shard_map/psum | solution.py:33
  324.0 16.1 %all-reduce.33 = (f32[1]{0:T(128)}, f32[1]{0:T(128)}) all-reduce(f32[1]{0:T(128)} %get-tuple-element.29, f32[1]{0:T(128)} %get-tuple-element.30), channel_id=1, replica_groups=mesh['tm'=8,'space_0'=8,'space_1'=12] {'space_1'}, use_global_device_ids=true, to_apply=%region_26.0 | all-reduce | flops 2 | bytes 16 | tf_op jit(solution)/shard_map/psum | solution.py:33
  344.0 4.3 collective-permute-start.15
  348.6 4.3 collective-permute-done.14
  352.9 1.5 collective-permute-done.15
  355.6 18.1 %all-reduce.38 = (f32[1]{0:T(128)}, f32[1]{0:T(128)}) all-reduce(f32[1]{0:T(128)} %bitcast.28, f32[1]{0:T(128)} %bitcast.29), channel_id=1, replica_groups=mesh['tm'=8,'space_0'=8,'space_1'=12] {'space_0'}, use_global_device_ids=true, to_apply=%region_31.0 | all-reduce | flops 2 | bytes 16 | tf_op jit(solution)/shard_map/psum | solution.py:33
  373.7 16.4 %all-reduce.32 = (f32[1]{0:T(128)}, f32[1]{0:T(128)}) all-reduce(f32[1]{0:T(128)} %get-tuple-element.27, f32[1]{0:T(128)} %get-tuple-element.28), channel_id=1, replica_groups=mesh['tm'=8,'space_0'=8,'space_1'=12] {'space_1'}, use_global_device_ids=true, to_apply=%region_32.0 | all-reduce | flops 2 | bytes 16 | tf_op jit(solution)/shard_map/psum | solution.py:33
  394.5 1.3 multiply_add_fusion.1
  396.9 64.9 %collective-permute-start.16 = (f32[2,1,512,256]{3,2,1,0:T(8,128)}, f32[2,1,512,256]{3,2,1,0:T(8,128)S(1)}, u32[]{:S(2)}, u32[]{:S(2)}) collective-permute-start(f32[2,1,512,256]{3,2,1,0:T(8,128)} %pad_maximum_fusion.1), channel_id=1, source_target_pairs={{0,96},{96,192},{192,288},{288,384},{384,480},{480,576},{576,672},... | collective-permute-start | bytes 3145736 | tf_op jit(solution)/shard_map/ppermute | solution.py:53
  463.0 10.8 %collective-permute-done.16 = f32[2,1,512,256]{3,2,1,0:T(8,128)S(1)} collective-permute-done((f32[2,1,512,256]{3,2,1,0:T(8,128)}, f32[2,1,512,256]{3,2,1,0:T(8,128)S(1)}, u32[]{:S(2)}, u32[]{:S(2)}) %collective-permute-start.16) | collective-permute-done | bytes 1048608 | tf_op jit(solution)/shard_map/ppermute | solution.py:53
  (115 shorter events, 23.2 us)
Async XLA Ops:
  0.6 14.3 %copy-start = (f32[1,3,1,512,256]{4,3,2,1,0:T(8,128)S(1)}, f32[1,3,1,512,256]{4,3,2,1,0:T(8,128)}, u32[]{:S(2)}) copy-start(f32[1,3,1,512,256]{4,3,2,1,0:T(8,128)} %param.7) | copy-start | bytes 4718596
  0.6 43.3 %collective-permute-start.1 = (f32[3,1,512,256]{3,2,1,0:T(8,128)}, f32[3,1,512,256]{3,2,1,0:T(8,128)S(1)}, u32[]{:S(2)}, u32[]{:S(2)}) collective-permute-start(f32[3,1,512,256]{3,2,1,0:T(8,128)} %bitcast.207), channel_id=1, source_target_pairs={{1,0},{2,1},{3,2},{4,3},{5,4},{6,5},{7,6},{8,7},{9,8},{10,9},{11,1... | collective-permute-start | bytes 4718600 | tf_op jit(solution)/shard_map/ppermute | solution.py:45
  2.1 41.9 %collective-permute-start.3 = (f32[3,1,512,256]{3,2,1,0:T(8,128)}, f32[3,1,512,256]{3,2,1,0:T(8,128)S(1)}, u32[]{:S(2)}, u32[]{:S(2)}) collective-permute-start(f32[3,1,512,256]{3,2,1,0:T(8,128)} %bitcast.208), channel_id=1, source_target_pairs={{0,1},{1,2},{2,3},{3,4},{4,5},{5,6},{6,7},{7,8},{8,9},{9,10},{10,1... | collective-permute-start | bytes 4718600 | tf_op jit(solution)/shard_map/ppermute | solution.py:44
  7.6 34.9 %collective-permute-start = (f32[1,512,256]{2,1,0:T(8,128)}, f32[1,512,256]{2,1,0:T(8,128)S(1)}, u32[]{:S(2)}, u32[]{:S(2)}) collective-permute-start(f32[1,512,256]{2,1,0:T(8,128)} %param.8), channel_id=1, source_target_pairs={{1,0},{2,1},{3,2},{4,3},{5,4},{6,5},{7,6},{8,7},{9,8},{10,9},{11,1... | collective-permute-start | bytes 1572872 | tf_op jit(solution)/shard_map/ppermute | solution.py:45
  8.9 34.6 %collective-permute-start.2 = (f32[1,512,256]{2,1,0:T(8,128)}, f32[1,512,256]{2,1,0:T(8,128)S(1)}, u32[]{:S(2)}, u32[]{:S(2)}) collective-permute-start(f32[1,512,256]{2,1,0:T(8,128)} %param.8), channel_id=1, source_target_pairs={{0,1},{1,2},{2,3},{3,4},{4,5},{5,6},{6,7},{7,8},{8,9},{9,10},{10,1... | collective-permute-start | bytes 1572872 | tf_op jit(solution)/shard_map/ppermute | solution.py:44
  43.9 36.2 %copy-start.1 = (f32[1,512,256]{2,1,0:T(8,128)}, f32[1,512,256]{2,1,0:T(8,128)S(1)}, u32[]{:S(2)}) copy-start(f32[1,512,256]{2,1,0:T(8,128)S(1)} %get-tuple-element.50) | copy-start | bytes 1572868
  43.9 36.2 %copy-start.7 = (f32[1,512,256]{2,1,0:T(8,128)}, f32[1,512,256]{2,1,0:T(8,128)S(1)}, u32[]{:S(2)}) copy-start(f32[1,512,256]{2,1,0:T(8,128)S(1)} %get-tuple-element.51) | copy-start | bytes 1572868
  43.9 36.2 %copy-start.13 = (f32[1,512,256]{2,1,0:T(8,128)}, f32[1,512,256]{2,1,0:T(8,128)S(1)}, u32[]{:S(2)}) copy-start(f32[1,512,256]{2,1,0:T(8,128)S(1)} %get-tuple-element.52) | copy-start | bytes 1572868
  43.9 36.2 %copy-start.29 = (f32[512,256]{1,0:T(8,128)}, f32[512,256]{1,0:T(8,128)S(1)}, u32[]{:S(2)}) copy-start(f32[512,256]{1,0:T(8,128)S(1)} %get-tuple-element.46) | copy-start | bytes 1572868
  46.5 33.6 %copy-start.19 = (f32[1,1,512,256]{3,2,1,0:T(8,128)}, f32[1,1,512,256]{3,2,1,0:T(8,128)S(1)}, u32[]{:S(2)}) copy-start(f32[1,1,512,256]{3,2,1,0:T(8,128)S(1)} %get-tuple-element.53) | copy-start | bytes 1572868
  46.6 33.6 %copy-start.21 = (f32[1,1,512,256]{3,2,1,0:T(8,128)}, f32[1,1,512,256]{3,2,1,0:T(8,128)S(1)}, u32[]{:S(2)}) copy-start(f32[1,1,512,256]{3,2,1,0:T(8,128)S(1)} %get-tuple-element.54) | copy-start | bytes 1572868
  46.6 32.6 %collective-permute-start.4 = (f32[2,1,512,256]{3,2,1,0:T(8,128)S(1)}, f32[2,1,512,256]{3,2,1,0:T(8,128)S(1)}, u32[]{:S(2)}, u32[]{:S(2)}) collective-permute-start(f32[2,1,512,256]{3,2,1,0:T(8,128)S(1)} %pad_maximum_fusion), channel_id=1, source_target_pairs={{1,0},{2,1},{3,2},{4,3},{5,4},{6,5},{7,6},{8,7},{9,8},{10,9},{11,1... | collective-permute-start | bytes 3145736 | tf_op jit(solution)/shard_map/ppermute | solution.py:45
  47.9 32.2 %collective-permute-start.5 = (f32[2,1,512,256]{3,2,1,0:T(8,128)S(1)}, f32[2,1,512,256]{3,2,1,0:T(8,128)S(1)}, u32[]{:S(2)}, u32[]{:S(2)}) collective-permute-start(f32[2,1,512,256]{3,2,1,0:T(8,128)S(1)} %pad_maximum_fusion), channel_id=1, source_target_pairs={{0,1},{1,2},{2,3},{3,4},{4,5},{5,6},{6,7},{7,8},{8,9},{9,10},{10,1... | collective-permute-start | bytes 3145736 | tf_op jit(solution)/shard_map/ppermute | solution.py:44
  60.4 19.8 %copy-start.38 = (f32[2]{0:T(128)S(1)}, f32[2]{0:T(128)}, u32[]{:S(2)}) copy-start(f32[2]{0:T(128)} %constant.14.clone) | copy-start | bytes 28
  132.5 15.9 %collective-permute-start.6 = (f32[2,1,512,256]{3,2,1,0:T(8,128)S(1)}, f32[2,1,512,256]{3,2,1,0:T(8,128)S(1)}, u32[]{:S(2)}, u32[]{:S(2)}) collective-permute-start(f32[2,1,512,256]{3,2,1,0:T(8,128)S(1)} %multiply_subtract_fusion.1), channel_id=1, source_target_pairs={{1,0},{2,1},{3,2},{4,3},{5,4},{6,5},{7,6},{8,7},{9,8},{10,9},{11,1... | collective-permute-start | bytes 3145736 | tf_op jit(solution)/shard_map/ppermute | solution.py:45
  133.8 16.1 %collective-permute-start.7 = (f32[2,1,512,256]{3,2,1,0:T(8,128)S(1)}, f32[2,1,512,256]{3,2,1,0:T(8,128)S(1)}, u32[]{:S(2)}, u32[]{:S(2)}) collective-permute-start(f32[2,1,512,256]{3,2,1,0:T(8,128)S(1)} %multiply_subtract_fusion.1), channel_id=1, source_target_pairs={{0,1},{1,2},{2,3},{3,4},{4,5},{5,6},{6,7},{7,8},{8,9},{9,10},{10,1... | collective-permute-start | bytes 3145736 | tf_op jit(solution)/shard_map/ppermute | solution.py:44
  139.4 10.5 %copy-start.2 = (f32[1,512,256]{2,1,0:T(8,128)S(1)}, f32[1,512,256]{2,1,0:T(8,128)}, u32[]{:S(2)}) copy-start(f32[1,512,256]{2,1,0:T(8,128)} %copy-done.1) | copy-start | bytes 1572868
  139.4 10.5 %copy-start.8 = (f32[1,512,256]{2,1,0:T(8,128)S(1)}, f32[1,512,256]{2,1,0:T(8,128)}, u32[]{:S(2)}) copy-start(f32[1,512,256]{2,1,0:T(8,128)} %copy-done.7) | copy-start | bytes 1572868
  139.4 10.5 %copy-start.14 = (f32[1,512,256]{2,1,0:T(8,128)S(1)}, f32[1,512,256]{2,1,0:T(8,128)}, u32[]{:S(2)}) copy-start(f32[1,512,256]{2,1,0:T(8,128)} %copy-done.13) | copy-start | bytes 1572868
  139.4 10.5 %copy-start.20 = (f32[1,1,512,256]{3,2,1,0:T(8,128)S(1)}, f32[1,1,512,256]{3,2,1,0:T(8,128)}, u32[]{:S(2)}) copy-start(f32[1,1,512,256]{3,2,1,0:T(8,128)} %copy-done.19) | copy-start | bytes 1572868
  139.4 10.5 %copy-start.22 = (f32[1,1,512,256]{3,2,1,0:T(8,128)S(1)}, f32[1,1,512,256]{3,2,1,0:T(8,128)}, u32[]{:S(2)}) copy-start(f32[1,1,512,256]{3,2,1,0:T(8,128)} %copy-done.21) | copy-start | bytes 1572868
  139.5 10.5 %copy-start.30 = (f32[512,256]{1,0:T(8,128)S(1)}, f32[512,256]{1,0:T(8,128)}, u32[]{:S(2)}) copy-start(f32[512,256]{1,0:T(8,128)} %copy-done.29) | copy-start | bytes 1572868
  139.5 10.5 %copy-start.31 = (f32[2,1,512,256]{3,2,1,0:T(8,128)S(1)}, f32[2,1,512,256]{3,2,1,0:T(8,128)}, u32[]{:S(2)}) copy-start(f32[2,1,512,256]{3,2,1,0:T(8,128)} %get-tuple-element.45) | copy-start | bytes 3145732
  188.6 11.5 %copy-start.24 = (f32[1,1,512,256]{3,2,1,0:T(8,128)}, f32[1,1,512,256]{3,2,1,0:T(8,128)S(1)}, u32[]{:S(2)}) copy-start(f32[1,1,512,256]{3,2,1,0:T(8,128)S(1)} %get-tuple-element.64) | copy-start | bytes 1572868
  188.6 10.0 %collective-permute-start.8 = (f32[1,1,512,256]{3,2,1,0:T(8,128)S(1)}, f32[1,1,512,256]{3,2,1,0:T(8,128)S(1)}, u32[]{:S(2)}, u32[]{:S(2)}) collective-permute-start(f32[1,1,512,256]{3,2,1,0:T(8,128)S(1)} %get-tuple-element.64), channel_id=1, source_target_pairs={{1,0},{2,1},{3,2},{4,3},{5,4},{6,5},{7,6},{8,7},{9,8},{10,9},{11,1... | collective-permute-start | bytes 1572872 | tf_op jit(solution)/shard_map/ppermute | solution.py:45
  189.9 10.2 %collective-permute-start.9 = (f32[1,1,512,256]{3,2,1,0:T(8,128)S(1)}, f32[1,1,512,256]{3,2,1,0:T(8,128)S(1)}, u32[]{:S(2)}, u32[]{:S(2)}) collective-permute-start(f32[1,1,512,256]{3,2,1,0:T(8,128)S(1)} %get-tuple-element.64), channel_id=1, source_target_pairs={{0,1},{1,2},{2,3},{3,4},{4,5},{5,6},{6,7},{7,8},{8,9},{9,10},{10,1... | collective-permute-start | bytes 1572872 | tf_op jit(solution)/shard_map/ppermute | solution.py:44
  194.0 6.1 %copy-start.3 = (f32[1,512,256]{2,1,0:T(8,128)S(1)}, f32[1,512,256]{2,1,0:T(8,128)}, u32[]{:S(2)}) copy-start(f32[1,512,256]{2,1,0:T(8,128)} %copy-done.1) | copy-start | bytes 1572868
  194.0 6.1 %copy-start.9 = (f32[1,512,256]{2,1,0:T(8,128)S(1)}, f32[1,512,256]{2,1,0:T(8,128)}, u32[]{:S(2)}) copy-start(f32[1,512,256]{2,1,0:T(8,128)} %copy-done.7) | copy-start | bytes 1572868
  194.0 6.1 %copy-start.15 = (f32[1,512,256]{2,1,0:T(8,128)S(1)}, f32[1,512,256]{2,1,0:T(8,128)}, u32[]{:S(2)}) copy-start(f32[1,512,256]{2,1,0:T(8,128)} %copy-done.13) | copy-start | bytes 1572868
  238.7 11.5 %copy-start.26 = (f32[1,1,512,256]{3,2,1,0:T(8,128)}, f32[1,1,512,256]{3,2,1,0:T(8,128)S(1)}, u32[]{:S(2)}) copy-start(f32[1,1,512,256]{3,2,1,0:T(8,128)S(1)} %multiply_subtract_fusion.5) | copy-start | bytes 1572868
  238.7 9.9 %collective-permute-start.10 = (f32[1,1,512,256]{3,2,1,0:T(8,128)S(1)}, f32[1,1,512,256]{3,2,1,0:T(8,128)S(1)}, u32[]{:S(2)}, u32[]{:S(2)}) collective-permute-start(f32[1,1,512,256]{3,2,1,0:T(8,128)S(1)} %multiply_subtract_fusion.5), channel_id=1, source_target_pairs={{1,0},{2,1},{3,2},{4,3},{5,4},{6,5},{7,6},{8,7},{9,8},{10,9},{11,1... | collective-permute-start | bytes 1572872 | tf_op jit(solution)/shard_map/ppermute | solution.py:45
  240.0 10.1 %collective-permute-start.11 = (f32[1,1,512,256]{3,2,1,0:T(8,128)S(1)}, f32[1,1,512,256]{3,2,1,0:T(8,128)S(1)}, u32[]{:S(2)}, u32[]{:S(2)}) collective-permute-start(f32[1,1,512,256]{3,2,1,0:T(8,128)S(1)} %multiply_subtract_fusion.5), channel_id=1, source_target_pairs={{0,1},{1,2},{2,3},{3,4},{4,5},{5,6},{6,7},{7,8},{8,9},{9,10},{10,1... | collective-permute-start | bytes 1572872 | tf_op jit(solution)/shard_map/ppermute | solution.py:44
  292.9 11.6 %copy-start.23 = (f32[1,1,512,256]{3,2,1,0:T(8,128)}, f32[1,1,512,256]{3,2,1,0:T(8,128)S(1)}, u32[]{:S(2)}) copy-start(f32[1,1,512,256]{3,2,1,0:T(8,128)S(1)} %get-tuple-element.40) | copy-start | bytes 1572868
  292.9 10.2 %collective-permute-start.12 = (f32[1,1,512,256]{3,2,1,0:T(8,128)S(1)}, f32[1,1,512,256]{3,2,1,0:T(8,128)S(1)}, u32[]{:S(2)}, u32[]{:S(2)}) collective-permute-start(f32[1,1,512,256]{3,2,1,0:T(8,128)S(1)} %get-tuple-element.40), channel_id=1, source_target_pairs={{1,0},{2,1},{3,2},{4,3},{5,4},{6,5},{7,6},{8,7},{9,8},{10,9},{11,1... | collective-permute-start | bytes 1572872 | tf_op jit(solution)/shard_map/ppermute | solution.py:45
  294.2 10.4 %collective-permute-start.13 = (f32[1,1,512,256]{3,2,1,0:T(8,128)S(1)}, f32[1,1,512,256]{3,2,1,0:T(8,128)S(1)}, u32[]{:S(2)}, u32[]{:S(2)}) collective-permute-start(f32[1,1,512,256]{3,2,1,0:T(8,128)S(1)} %get-tuple-element.40), channel_id=1, source_target_pairs={{0,1},{1,2},{2,3},{3,4},{4,5},{5,6},{6,7},{7,8},{8,9},{9,10},{10,1... | collective-permute-start | bytes 1572872 | tf_op jit(solution)/shard_map/ppermute | solution.py:44
  298.5 6.0 %copy-start.5 = (f32[1,512,256]{2,1,0:T(8,128)S(1)}, f32[1,512,256]{2,1,0:T(8,128)}, u32[]{:S(2)}) copy-start(f32[1,512,256]{2,1,0:T(8,128)} %copy-done.1) | copy-start | bytes 1572868
  298.5 6.0 %copy-start.11 = (f32[1,512,256]{2,1,0:T(8,128)S(1)}, f32[1,512,256]{2,1,0:T(8,128)}, u32[]{:S(2)}) copy-start(f32[1,512,256]{2,1,0:T(8,128)} %copy-done.7) | copy-start | bytes 1572868
  298.6 6.0 %copy-start.17 = (f32[1,512,256]{2,1,0:T(8,128)S(1)}, f32[1,512,256]{2,1,0:T(8,128)}, u32[]{:S(2)}) copy-start(f32[1,512,256]{2,1,0:T(8,128)} %copy-done.13) | copy-start | bytes 1572868
  342.7 11.7 %copy-start.25 = (f32[1,1,512,256]{3,2,1,0:T(8,128)}, f32[1,1,512,256]{3,2,1,0:T(8,128)S(1)}, u32[]{:S(2)}) copy-start(f32[1,1,512,256]{3,2,1,0:T(8,128)S(1)} %multiply_subtract_fusion.4) | copy-start | bytes 1572868
  342.7 10.2 %collective-permute-start.14 = (f32[1,1,512,256]{3,2,1,0:T(8,128)S(1)}, f32[1,1,512,256]{3,2,1,0:T(8,128)S(1)}, u32[]{:S(2)}, u32[]{:S(2)}) collective-permute-start(f32[1,1,512,256]{3,2,1,0:T(8,128)S(1)} %multiply_subtract_fusion.4), channel_id=1, source_target_pairs={{1,0},{2,1},{3,2},{4,3},{5,4},{6,5},{7,6},{8,7},{9,8},{10,9},{11,1... | collective-permute-start | bytes 1572872 | tf_op jit(solution)/shard_map/ppermute | solution.py:45
  344.0 10.4 %collective-permute-start.15 = (f32[1,1,512,256]{3,2,1,0:T(8,128)S(1)}, f32[1,1,512,256]{3,2,1,0:T(8,128)S(1)}, u32[]{:S(2)}, u32[]{:S(2)}) collective-permute-start(f32[1,1,512,256]{3,2,1,0:T(8,128)S(1)} %multiply_subtract_fusion.4), channel_id=1, source_target_pairs={{0,1},{1,2},{2,3},{3,4},{4,5},{5,6},{6,7},{7,8},{8,9},{9,10},{10,1... | collective-permute-start | bytes 1572872 | tf_op jit(solution)/shard_map/ppermute | solution.py:44
  348.4 6.0 %copy-start.6 = (f32[1,512,256]{2,1,0:T(8,128)S(1)}, f32[1,512,256]{2,1,0:T(8,128)}, u32[]{:S(2)}) copy-start(f32[1,512,256]{2,1,0:T(8,128)} %copy-done.1) | copy-start | bytes 1572868
  348.4 6.0 %copy-start.12 = (f32[1,512,256]{2,1,0:T(8,128)S(1)}, f32[1,512,256]{2,1,0:T(8,128)}, u32[]{:S(2)}) copy-start(f32[1,512,256]{2,1,0:T(8,128)} %copy-done.7) | copy-start | bytes 1572868
  355.6 40.2 %copy-start.34 = (f32[1,1,512,256]{3,2,1,0:T(8,128)S(1)}, f32[1,1,512,256]{3,2,1,0:T(8,128)}, u32[]{:S(2)}) copy-start(f32[1,1,512,256]{3,2,1,0:T(8,128)} %get-tuple-element.63) | copy-start | bytes 1572868
  395.8 66.0 %copy-start.33 = (f32[1,1,512,256]{3,2,1,0:T(8,128)S(1)}, f32[1,1,512,256]{3,2,1,0:T(8,128)}, u32[]{:S(2)}) copy-start(f32[1,1,512,256]{3,2,1,0:T(8,128)} %get-tuple-element.65) | copy-start | bytes 1572868
  395.8 66.0 %copy-start.37 = (f32[1,1,512,256]{3,2,1,0:T(8,128)S(1)}, f32[1,1,512,256]{3,2,1,0:T(8,128)}, u32[]{:S(2)}) copy-start(f32[1,1,512,256]{3,2,1,0:T(8,128)} %get-tuple-element.41) | copy-start | bytes 1572868
  396.9 76.9 %collective-permute-start.16 = (f32[2,1,512,256]{3,2,1,0:T(8,128)}, f32[2,1,512,256]{3,2,1,0:T(8,128)S(1)}, u32[]{:S(2)}, u32[]{:S(2)}) collective-permute-start(f32[2,1,512,256]{3,2,1,0:T(8,128)} %pad_maximum_fusion.1), channel_id=1, source_target_pairs={{0,96},{96,192},{192,288},{288,384},{384,480},{480,576},{576,672},... | collective-permute-start | bytes 3145736 | tf_op jit(solution)/shard_map/ppermute | solution.py:53
  461.8 12.0 %copy-start.36 = (f32[1,1,512,256]{3,2,1,0:T(8,128)S(1)}, f32[1,1,512,256]{3,2,1,0:T(8,128)}, u32[]{:S(2)}) copy-start(f32[1,1,512,256]{3,2,1,0:T(8,128)} %param.6) | copy-start | bytes 1572868
  (8 other events, 29.8 us)
where the time goes:
time: 476 us; the launch traced here: 475 us
  blocking collectives  218 us (46%)
  starting transfers between devices  119 us (25%)
  waiting for transfers between devices  90.1 us (19%)
  other arithmetic  28.4 us (6%)
  between operations  12.6 us (3%)
  local copies, waits for them, and re-layouts  6.67 us (1%)
    psum x12, blocking collectives, one_axis_at_a_time(): value = lax.psum(value, axis)  218 us
    ppermute x8, waiting for transfers between devices, padded_2(): after = lax.ppermute(leading, axis, down)  70 us
    ppermute x1, starting transfers between devices, from_behind(): return lax.ppermute(block, axis, route)  64.9 us
    ppermute x8, starting transfers between devices, padded_2(): before = lax.ppermute(last, axis, up)  43.6 us
    ppermute x1, waiting for transfers between devices, from_behind(): return lax.ppermute(block, axis, route)  10.8 us
    ppermute x8, starting transfers between devices, padded_2(): after = lax.ppermute(leading, axis, down)  10.4 us
    reduce_sum x6, other arithmetic, inner(): return jnp.sum(left * right, axis=(1, 2, 3))  9.93 us
  transfers between devices with their start and end apart: 17, of which 15 were waited for; matrix products, arithmetic and copies ran while one was open for 1% of the time, Pallas kernels for 0%

commit v1 on v0

v1 whole, which is shorter than its diff:
```python
import functools
import math

import jax
import jax.numpy as jnp
from jax import lax
from jax.experimental import pallas as pl
from jax.experimental.pallas import tpu as pltpu
from jax.sharding import Mesh
from jax.sharding import PartitionSpec as P

MESH = pl.DeviceIdType.MESH
SPACE = ("y", "z")
ROWS_Y = 8
STEP = 2.0
ROOT_SIX = math.sqrt(6.0)
NODE_TIMES = [(4.0 - ROOT_SIX) / 10.0, (4.0 + ROOT_SIX) / 10.0, 1.0]
COLLOC = [
    [
        (88.0 - 7.0 * ROOT_SIX) / 360.0,
        (296.0 - 169.0 * ROOT_SIX) / 1800.0,
        (-2.0 + 3.0 * ROOT_SIX) / 225.0,
    ],
    [
        (296.0 + 169.0 * ROOT_SIX) / 1800.0,
        (88.0 + 7.0 * ROOT_SIX) / 360.0,
        (-2.0 - 3.0 * ROOT_SIX) / 225.0,
    ],
    [(16.0 - ROOT_SIX) / 36.0, (16.0 + ROOT_SIX) / 36.0, 1.0 / 9.0],
]
WEIGHT = [
    [STEP * (COLLOC[m][j] - (COLLOC[m - 1][j] if m else 0.0)) for j in range(3)] for m in range(3)
]
WIDTH = [STEP * (NODE_TIMES[m] - (NODE_TIMES[m - 1] if m else 0.0)) for m in range(3)]
PAD = 8
BLOCK = 32
CHUNKS = 4

PADDED = ["k", "u0", "u1", "u2", "a", "b", "d", "la", "v2", "v3", "vc"]
PLANES = ["s", "wxm", "wxp", "wym", "wyp", "wzm", "wzp", "dg", "lb", "ld", "lla", "lv2"]
PLANES += ["r2", "r3", "rc", "hv3", "hvc", "xu", "xrc", "xvc", "xr3", "xv3"]
PLANES += ["o0", "o1", "o2", "ons", "onc"]
SIDES = ["k", "u0", "u1", "u2", "a", "b", "d", "la", "v2"]


def kernel(dims, start_hbm, old_hbm, kappa_hbm, fine_hbm, ns_hbm, nc_hbm, padded, planes, sides,
           tiles, ztiles, zslots, yslots, xslots, send, recv, gsend, grecv, local):
    nt, ny, nz, rows, cols = dims
    chunk = rows // CHUNKS
    me_t, me_y, me_z = lax.axis_index("tm"), lax.axis_index("y"), lax.axis_index("z")
    place = me_y * nz + me_z
    slabs = ny * nz

    def chain(shift):
        other = lax.rem(place + (slabs + shift), slabs)
        return (me_t, lax.div(other, nz), lax.rem(other, nz))

    after, before = chain(1), chain(-1)
    next_t = lax.rem(me_t + 1, nt)
    last_t = lax.rem(me_t + (nt - 1), nt)

    def z_peer(k):
        return (me_t, me_y, lax.rem(me_z + k, nz))

    def y_peer(k, t=me_t):
        return (t, lax.rem(me_y + k, ny), me_z)

    def t_peer(k):
        return (lax.rem(me_t + k, nt), me_y, me_z)

    pad = {name: padded.at[i] for i, name in enumerate(PADDED)}
    plane = {name: planes.at[i] for i, name in enumerate(PLANES)}
    side = {name: sides.at[i] for i, name in enumerate(SIDES)}

    def inner(name, first=0, count=rows):
        return pad[name].at[pl.ds(PAD + first, count), :]

    loads = [(kappa_hbm, "k"), (old_hbm.at[0], "u0"), (old_hbm.at[1], "u1"), (old_hbm.at[2], "u2")]
    copies = [pltpu.make_async_copy(src, inner(name), local.at[i]) for i, (src, name) in enumerate(loads)]
    copies.append(pltpu.make_async_copy(start_hbm, plane["s"], local.at[4]))
    for copy in copies:
        copy.start()
    barrier = pltpu.get_barrier_semaphore()
    greeted = [after, before]
    greeted += [z_peer(k) for k in range(1, nz)]
    greeted += [y_peer(k) for k in range(1, ny)]
    greeted += [t_peer(k) for k in range(1, nt)]
    greeted += [y_peer(k, last_t) for k in range(ny)]
    for device in greeted:
        pl.semaphore_signal(barrier, inc=1, device_id=device, device_id_type=MESH)
    edge = jnp.zeros((PAD, cols), jnp.float32)
    for name in PADDED:
        pad[name][pl.ds(0, PAD), :] = edge
        pad[name][pl.ds(PAD + rows, PAD), :] = edge
    for copy in copies:
        copy.wait()
    pl.semaphore_wait(barrier, len(greeted))

    started = []

    def put(src, dst, device):
        i = len(started)
        copy = pltpu.make_async_remote_copy(
            src_ref=src, dst_ref=dst, send_sem=send.at[i], recv_sem=recv.at[i],
            device_id=device, device_id_type=MESH,
        )
        copy.start()
        started.append(copy)
        return copy

    def swap(name, c):
        here = inner(name, c * chunk, chunk)
        there = pl.ds(c * chunk, chunk)
        return [
            put(here, side[name].at[0, there, :], after),
            put(here, side[name].at[1, there, :], before),
        ]

    def swap_half(name, c, second):
        here = inner(name, c * chunk, chunk)
        there = pl.ds(c * chunk, chunk)
        up = (c < CHUNKS // 2) != second
        return [put(here, side[name].at[0 if up else 1, there, :], after if up else before)]

    def give_half(name, c):
        up = c < CHUNKS // 2
        here = inner(name, c * chunk, chunk)
        there = plane["h" + name].at[pl.ds(c * chunk, chunk), :]
        return [put(here, there, after if up else before)]

    def arrive(batch):
        for copy in batch:
            copy.wait_recv()

    share = rows // nt
    own = pl.multiple_of(me_t * share, share)
    mine = pl.ds(own, share)
    k_src = pad["k"].at[pl.ds(pl.multiple_of(PAD + own, PAD), share), :]
    k_in = [put(k_src, side["k"].at[0, mine, :], after), put(k_src, side["k"].at[1, mine, :], before)]
    u_in = []
    for c in range(CHUNKS):
        u_in.append([swap("u%d" % j, c) for j in range(3)])
    put_u = put(inner("u2"), plane["xu"], (next_t, me_y, me_z))
    arrive(k_in)
    for s in range(2):
        block = side["k"].at[s, mine, :]
        for k in range(1, nt):
            pltpu.make_async_remote_copy(
                src_ref=block, dst_ref=block, send_sem=gsend.at[0], recv_sem=grecv.at[0],
                device_id=t_peer(k), device_id_type=MESH,
            ).start()
    spread = side["k"].at[:, pl.ds(0, share * (nt - 1)), :]
    shared = pltpu.make_async_remote_copy(
        src_ref=spread, dst_ref=spread, send_sem=gsend.at[0], recv_sem=grecv.at[0],
        device_id=after, device_id_type=MESH,
    )
    shared.wait_recv()

    lane = lax.broadcasted_iota(jnp.int32, (BLOCK, cols), 1)
    first_lane, last_lane = lane == 0, lane == cols - 1
    zero = jnp.zeros((BLOCK, cols), jnp.float32)

    def to_right(x):
        return pltpu.roll(x, cols - 1, 1)

    def to_left(x):
        return pltpu.roll(x, 1, 1)

    def at(r):
        return pl.ds(r, BLOCK)

    def column(name, r):
        x = pad[name][pl.ds(r, BLOCK + 2 * PAD), :]
        return x[PAD:PAD + BLOCK], x[PAD - 1:PAD + BLOCK - 1], x[PAD + 1:PAD + BLOCK + 1]

    def sweep(first, count, body, carry):
        def step(i, carry):
            return body(pl.multiple_of(first + i * BLOCK, BLOCK), carry)

        return lax.fori_loop(0, count // BLOCK, step, carry)

    def weights(r, carry):
        k, k_down, k_up = column("k", r)
        row = lax.broadcasted_iota(jnp.int32, (BLOCK, cols), 0) + r
        k_before = jnp.where(place == 0, zero, side["k"][0, at(r), :])
        k_after = jnp.where(place == slabs - 1, zero, side["k"][1, at(r), :])
        faces = [
            0.5 * (k + k_before),
            0.5 * (k + k_after),
            0.5 * (k + k_down),
            0.5 * (k + k_up),
            0.5 * (k + jnp.where(first_lane, zero, to_left(k))),
            0.5 * (k + jnp.where(last_lane, zero, to_right(k))),
        ]
        total = faces[1] + faces[0] + faces[3] + faces[2] + faces[5] + faces[4]
        plane["dg"][at(r), :] = -total
        plane["wxm"][at(r), :] = jnp.where(place == 0, zero, faces[0])
        plane["wxp"][at(r), :] = jnp.where(place == slabs - 1, zero, faces[1])
        plane["wym"][at(r), :] = jnp.where(row == 0, zero, faces[2])
        plane["wyp"][at(r), :] = jnp.where(row == rows - 1, zero, faces[3])
        plane["wzm"][at(r), :] = jnp.where(first_lane, zero, faces[4])
        plane["wzp"][at(r), :] = jnp.where(last_lane, zero, faces[5])
        return carry

    sweep(0, rows, weights, 0)

    def heat(name, r):
        mid, down, up = column(name, r)
        out = plane["wxp"][at(r), :] * side[name][1, at(r), :]
        out = out + plane["wxm"][at(r), :] * side[name][0, at(r), :]
        out = out + plane["wyp"][at(r), :] * up + plane["wym"][at(r), :] * down
        out = out + plane["wzp"][at(r), :] * to_right(mid) + plane["wzm"][at(r), :] * to_left(mid)
        return mid, out + plane["dg"][at(r), :] * mid

    def fold(x):
        return jnp.sum(x.reshape(BLOCK // 8, 8, cols), axis=0)

    nothing = jnp.zeros((8, cols), jnp.float32)

    def quadratic(name, beside, weight, r):
        mid, _, up = column(name, r)
        twice = plane[weight][at(r), :] * beside[at(r), :]
        twice = twice + plane["wyp"][at(r), :] * up + plane["wzp"][at(r), :] * to_right(mid)
        return fold(mid * (twice + twice + plane["dg"][at(r), :] * mid))

    def moments(name, beside, c):
        weight = "wxm" if c < CHUNKS // 2 else "wxp"
        beside = beside(0 if c < CHUNKS // 2 else 1)
        return sweep(c * chunk, chunk, lambda r, acc: acc + quadratic(name, beside, weight, r), nothing)

    def lanes(acc):
        both = acc[:, 0:128]
        for i in range(1, cols // 128):
            both = both + acc[:, i * 128:(i + 1) * 128]
        return jnp.sum(both, axis=0, keepdims=True)

    def burst(src, slots, base, devices, sem):
        for k, device in enumerate(devices):
            pltpu.make_async_remote_copy(
                src_ref=src, dst_ref=slots.at[base + k], send_sem=gsend.at[sem], recv_sem=grecv.at[sem],
                device_id=device, device_id_type=MESH,
            ).start()
        whole = slots.at[pl.ds(base, len(devices))]
        return pltpu.make_async_remote_copy(
            src_ref=whole, dst_ref=whole, send_sem=gsend.at[sem], recv_sem=grecv.at[sem],
            device_id=after, device_id_type=MESH,
        )

    bursts = [shared]

    def reduce_z(n, accs):
        accs = accs + [nothing] * (8 - len(accs))
        tiles[n] = jnp.concatenate([lanes(acc) for acc in accs], axis=0)
        waits = burst(tiles.at[n], zslots.at[n], 0, [z_peer(k) for k in range(1, nz)], 1 + 3 * n)
        bursts.append(waits)
        return waits

    def reduce_y(n, waits, onward=False):
        waits.wait_recv()
        total = tiles[n]
        for k in range(nz - 1):
            total = total + zslots[n, k]
        ztiles[n] = total
        out = [burst(ztiles.at[n], yslots.at[n], 0, [y_peer(k) for k in range(1, ny)], 2 + 3 * n)]
        if onward:
            out.append(burst(ztiles.at[n], xslots, 0, [y_peer(k, next_t) for k in range(ny)], 3 + 3 * n))
        bursts.extend(out)
        return out

    def total_own(n, waits):
        waits.wait_recv()
        total = ztiles[n]
        for k in range(ny - 1):
            total = total + yslots[n, k]
        return jnp.sum(total, axis=1, keepdims=True)

    def total_last(waits):
        waits.wait_recv()
        total = xslots[0]
        for k in range(1, ny):
            total = total + xslots[k]
        return jnp.sum(total, axis=1, keepdims=True)

    def factors(sums, first, h):
        s0, s1, s2, s3 = [sums[first + i:first + i + 1, :] for i in range(4)]
        sigma = s1 / s0
        spread = jnp.maximum(s2 - s1 * sigma, 1e-30)
        bent = s3 - sigma * (s2 + s2) + sigma * sigma * s1
        one = s0 / (s0 - h * s1)
        part = spread / s0
        two = 1.0 / jnp.maximum(1.0 - h * bent / spread - one * (h * h) * part, 1.0)
        slope = (one * h) * (one * h) * part
        c1 = one * two * h
        c0 = one + two * slope - c1 * sigma
        return c0, c1

    def first_fields(r, carry):
        mids, images = zip(*[heat("u%d" % j, r) for j in range(3)])
        begin = plane["s"][at(r), :]
        leads = [begin - mids[0], mids[0] - mids[1], mids[1] - mids[2]]
        rc = None
        for m, name in enumerate(["a", "b", "d"]):
            value = leads[m]
            for j in range(3):
                value = value + WEIGHT[m][j] * images[j]
            pad[name][pl.ds(PAD + r, BLOCK), :] = value
            rc = value if rc is None else rc + value
        plane["rc"][at(r), :] = rc
        return carry

    a_in, b_in, d_in, la_in = [], [], [], []
    for c in range(CHUNKS):
        for j in range(3):
            arrive(u_in[c][j])
        sweep(c * chunk, chunk, first_fields, 0)
        a_in.append(swap("a", c))
    put_rc = put(plane["rc"], plane["xrc"], (next_t, me_y, me_z))
    for c in range(CHUNKS):
        b_in.append(swap("b", c))

    def first_heat(r, carry):
        s0, s1, s2 = carry
        mid, out = heat("a", r)
        pad["la"][pl.ds(PAD + r, BLOCK), :] = out
        return s0 + fold(mid * mid), s1 + fold(mid * out), s2 + fold(out * out)

    sums = (nothing,) * 3
    for c in range(CHUNKS):
        arrive(a_in[c])
        sums = sweep(c * chunk, chunk, first_heat, sums)
        la_in.append(swap("la", c))
    d_in.append(swap("d", 0))

    def second_field(r, carry):
        plane["lb"][at(r), :] = heat("b", r)[1]
        return carry

    for c in range(CHUNKS):
        arrive(b_in[c])
        sweep(c * chunk, chunk, second_field, 0)

    def second_heat(r, carry):
        mid, out = heat("la", r)
        plane["lla"][at(r), :] = out
        return carry + fold(mid * out)

    s3 = nothing
    for c in range(CHUNKS):
        arrive(la_in[c])
        s3 = sweep(c * chunk, chunk, second_heat, s3)
    z_wait = reduce_z(0, list(sums) + [s3])
    for c in range(1, CHUNKS):
        d_in.append(swap("d", c))

    def third_field(r, carry):
        s0, s1, s2 = carry
        ld = heat("d", r)[1]
        rc = plane["rc"][at(r), :]
        vc = pad["la"][pl.ds(PAD + r, BLOCK), :] + plane["lb"][at(r), :] + ld
        plane["ld"][at(r), :] = ld
        pad["vc"][pl.ds(PAD + r, BLOCK), :] = vc
        return s0 + fold(rc * rc), s1 + fold(rc * vc), s2 + fold(vc * vc)

    coarse = (nothing,) * 3
    arrive(d_in[0])
    coarse = sweep(0, chunk, third_field, coarse)
    (y_wait,) = reduce_y(0, z_wait)
    if CHUNKS > 2:
        arrive(d_in[1])
        coarse = sweep(chunk, chunk, third_field, coarse)
    c0, c1 = factors(total_own(0, y_wait), 0, WIDTH[0])

    def second_node(r, carry):
        s0, s1, s2 = carry
        at_pad = pl.ds(PAD + r, BLOCK)
        a, la, lla = pad["a"][at_pad, :], pad["la"][at_pad, :], plane["lla"][at(r), :]
        move = c0 * a + c1 * la
        plane["o0"][at(r), :] = pad["u0"][at_pad, :] + move
        r2 = pad["b"][at_pad, :] + move
        v2 = plane["lb"][at(r), :] + c0 * la + c1 * lla
        plane["r2"][at(r), :] = r2
        pad["v2"][at_pad, :] = v2
        return s0 + fold(r2 * r2), s1 + fold(r2 * v2), s2 + fold(v2 * v2)

    sums = (nothing,) * 3
    v_in = {}
    order = [i // 2 + (i % 2) * (CHUNKS // 2) for i in range(CHUNKS)]
    for c in order:
        sums = sweep(c * chunk, chunk, second_node, sums)
        v_in[c] = swap_half("v2", c, False)
    w_in = {}
    for c in order[:2]:
        w_in[c] = swap_half("v2", c, True)
    outs = [pltpu.make_async_copy(plane["o0"], fine_hbm.at[0], local.at[5])]
    outs[0].start()
    for c in range(2 if CHUNKS > 2 else 1, CHUNKS):
        arrive(d_in[c])
        coarse = sweep(c * chunk, chunk, third_field, coarse)
    put_vc = put(inner("vc"), plane["xvc"], (next_t, me_y, me_z))
    s3 = nothing
    for c in order:
        arrive(v_in[c])
        s3 = s3 + moments("v2", lambda s: side["v2"].at[s], c)
    z_wait = reduce_z(1, list(sums) + [s3])
    for c in order[2:]:
        w_in[c] = swap_half("v2", c, True)
    vc_in = {c: give_half("vc", c) for c in order}

    def third_heat(r, carry):
        plane["lv2"][at(r), :] = heat("v2", r)[1]
        return carry

    for c in order[:2]:
        arrive(w_in[c])
        sweep(c * chunk, chunk, third_heat, 0)
    (y_wait,) = reduce_y(1, z_wait)
    for c in order[2:]:
        arrive(w_in[c])
        sweep(c * chunk, chunk, third_heat, 0)
    e0, e1 = factors(total_own(1, y_wait), 0, WIDTH[1])

    def third_node(r, carry):
        s0, s1, s2 = carry
        at_pad = pl.ds(PAD + r, BLOCK)
        r2, v2, lv2 = plane["r2"][at(r), :], pad["v2"][at_pad, :], plane["lv2"][at(r), :]
        move = e0 * r2 + e1 * v2
        plane["o1"][at(r), :] = pad["u1"][at_pad, :] + move
        r3 = pad["d"][at_pad, :] + move
        v3 = plane["ld"][at(r), :] + e0 * v2 + e1 * lv2
        plane["r3"][at(r), :] = r3
        pad["v3"][at_pad, :] = v3
        return s0 + fold(r3 * r3), s1 + fold(r3 * v3), s2 + fold(v3 * v3)

    sums = (nothing,) * 3
    v3_in = {}
    for c in order:
        sums = sweep(c * chunk, chunk, third_node, sums)
        v3_in[c] = give_half("v3", c)
    put_r3 = put(plane["r3"], plane["xr3"], (next_t, me_y, me_z))
    put_v3 = put(inner("v3"), plane["xv3"], (next_t, me_y, me_z))
    outs.append(pltpu.make_async_copy(plane["o1"], fine_hbm.at[1], local.at[6]))
    outs[1].start()
    coarse3 = nothing
    for c in order:
        arrive(vc_in[c])
        coarse3 = coarse3 + moments("vc", lambda s: plane["hvc"], c)
    s3 = nothing
    for c in order:
        arrive(v3_in[c])
        s3 = s3 + moments("v3", lambda s: plane["hv3"], c)
    z_wait = reduce_z(2, list(sums) + [s3] + list(coarse) + [coarse3])
    y_wait, x_wait = reduce_y(2, z_wait, onward=True)
    for copy in (put_u, put_rc, put_vc, put_r3, put_v3):
        copy.wait_recv()
    g0, g1 = factors(total_own(2, y_wait), 0, WIDTH[2])

    def last_node(r, carry):
        at_pad = pl.ds(PAD + r, BLOCK)
        move = g0 * plane["r3"][at(r), :] + g1 * pad["v3"][at_pad, :]
        plane["o2"][at(r), :] = pad["u2"][at_pad, :] + move
        return carry

    sweep(0, rows, last_node, 0)
    outs.append(pltpu.make_async_copy(plane["o2"], fine_hbm.at[2], local.at[7]))
    outs[2].start()
    sums = total_last(x_wait)
    p0, p1 = factors(sums, 0, WIDTH[2])
    q0, q1 = factors(sums, 4, STEP)

    def next_slice(r, carry):
        begin, guess = plane["s"][at(r), :], plane["xu"][at(r), :]
        fine = guess + (p0 * plane["xr3"][at(r), :] + p1 * plane["xv3"][at(r), :])
        coarse = guess + (q0 * plane["xrc"][at(r), :] + q1 * plane["xvc"][at(r), :])
        plane["ons"][at(r), :] = jnp.where(me_t == 0, begin, fine)
        plane["onc"][at(r), :] = jnp.where(me_t == 0, begin, coarse)
        return carry

    sweep(0, rows, next_slice, 0)
    outs.append(pltpu.make_async_copy(plane["ons"], ns_hbm, local.at[8]))
    outs.append(pltpu.make_async_copy(plane["onc"], nc_hbm, local.at[9]))
    for copy in outs[3:]:
        copy.start()
    for copy in started:
        copy.wait_send()
    for waits in bursts:
        waits.wait_send()
    for copy in outs:
        copy.wait()


def copies_needed():
    return 2 + 6 * CHUNKS + 5 * 2 * CHUNKS + 2 * CHUNKS + 5


def on_device(dims, start_value, old_nodes, diffusivity):
    nt, ny, nz, rows, cols = dims
    anywhere = pl.BlockSpec(memory_space=pl.ANY)
    plane = jax.ShapeDtypeStruct((rows, cols), jnp.float32)
    fine, following, coarse = pl.pallas_call(
        functools.partial(kernel, dims),
        out_shape=(jax.ShapeDtypeStruct((3, rows, cols), jnp.float32), plane, plane),
        in_specs=[anywhere] * 3,
        out_specs=(anywhere,) * 3,
        scratch_shapes=[
            pltpu.VMEM((len(PADDED), rows + 2 * PAD, cols), jnp.float32),
            pltpu.VMEM((len(PLANES), rows, cols), jnp.float32),
            pltpu.VMEM((len(SIDES), 2, rows, cols), jnp.float32),
            pltpu.VMEM((3, 8, 128), jnp.float32),
            pltpu.VMEM((3, 8, 128), jnp.float32),
            pltpu.VMEM((3, nz - 1, 8, 128), jnp.float32),
            pltpu.VMEM((3, ny - 1, 8, 128), jnp.float32),
            pltpu.VMEM((ny, 8, 128), jnp.float32),
            pltpu.SemaphoreType.DMA((copies_needed(),)),
            pltpu.SemaphoreType.DMA((copies_needed(),)),
            pltpu.SemaphoreType.DMA((10,)),
            pltpu.SemaphoreType.DMA((10,)),
            pltpu.SemaphoreType.DMA((10,)),
        ],
        compiler_params=pltpu.CompilerParams(
            collective_id=0, has_side_effects=True, vmem_limit_bytes=60 * 1024 * 1024
        ),
    )(start_value.reshape(rows, cols), old_nodes.reshape(3, rows, cols), diffusivity.reshape(rows, cols))
    return (
        fine.reshape(1, 3, 1, rows, cols),
        following.reshape(1, 1, rows, cols),
        coarse.reshape(1, 1, rows, cols),
    )


def build(split, rows, cols):
    dims = (split.shape["tm"], split.shape["y"], split.shape["z"], rows, cols)
    in_specs = (P("tm", SPACE, None, None), P("tm", None, SPACE, None, None), P(SPACE, None, None))
    out_specs = (
        P("tm", None, SPACE, None, None),
        P("tm", SPACE, None, None),
        P("tm", SPACE, None, None),
    )
    return jax.shard_map(
        functools.partial(on_device, dims), mesh=split, in_specs=in_specs, out_specs=out_specs,
        check_vma=False,
    )


def solution(mesh):
    split = Mesh(
        mesh.devices.reshape(mesh.shape["tm"], ROWS_Y, mesh.shape["space"] // ROWS_Y), ("tm",) + SPACE
    )
    return build(split, 512, 256)
```

time: 476 us -> 160 us (0.34)
  the two profiles are of different devices: /device:TPU:1 before, /device:TPU:6 now
where the time goes in v1:
time: 160 us
  Pallas kernels  155 us (97%)
  local copies, waits for them, and re-layouts  4.33 us (3%)
    pallas_call x1, Pallas kernels, on_device(): pl.pallas_call(functools.partial(kernel, dims), out_shape=(jax.ShapeDtype...  155 us
    unnamed x7, local copies, waits for them, and re-layouts  4.33 us

profile of v1, /device:TPU:6, one launch (start us, length us, event | category | flops | bytes accessed | tf_op | source)
XLA Modules:
  0.0 159.7 jit_solution(17383897802513578437)
XLA Ops:
  0.6 154.8 %shard_map.58 = (f32[3,512,256]{2,1,0:T(8,128)}, f32[512,256]{1,0:T(8,128)}, f32[512,256]{1,0:T(8,128)}) custom-call(f32[512,256]{1,0:T(8,128)} %bitcast.10, f32[3,512,256]{2,1,0:T(8,128)} %bitcast.8, f32[512,256]{1,0:T(8,128)} %bitcast.11), custom_call_target="tpu_custom_call" | custom-call | tf_op jit(solution)/shard_map/pallas_call | solution.py:499
  155.4 0.0 copy-start.1
  155.4 0.0 copy-start
  155.4 2.7 %copy.10 = f32[1,3,1,512,256]{4,3,2,1,0:T(8,128)} copy(f32[1,3,1,512,256]{4,3,2,1,0:T(8,128)} %bitcast.9) | data formatting | bytes 3145728
  158.2 0.0 copy-done.1
  158.2 0.8 copy.11
  159.0 0.0 copy-done
  159.0 0.8 copy.12
Async XLA Ops:
  155.4 2.8 %copy-start.1 = (f32[512,256]{1,0:T(8,128)S(1)}, f32[512,256]{1,0:T(8,128)}, u32[]{:S(2)}) copy-start(f32[512,256]{1,0:T(8,128)} %get-tuple-element.7) | copy-start | bytes 1572868
  155.4 3.5 %copy-start = (f32[512,256]{1,0:T(8,128)S(1)}, f32[512,256]{1,0:T(8,128)}, u32[]{:S(2)}) copy-start(f32[512,256]{1,0:T(8,128)} %get-tuple-element.8) | copy-start | bytes 1572868

commit v2 on v1

--- a/solution.py
+++ b/solution.py
@@ -34,16 +34,15 @@
 WIDTH = [STEP * (NODE_TIMES[m] - (NODE_TIMES[m - 1] if m else 0.0)) for m in range(3)]
 PAD = 8
 BLOCK = 32
-CHUNKS = 4
+CHUNKS = 8
 
 PADDED = ["k", "u0", "u1", "u2", "a", "b", "d", "la", "v2", "v3", "vc"]
 PLANES = ["s", "wxm", "wxp", "wym", "wyp", "wzm", "wzp", "dg", "lb", "ld", "lla", "lv2"]
 PLANES += ["r2", "r3", "rc", "hv3", "hvc", "xu", "xrc", "xvc", "xr3", "xv3"]
-PLANES += ["o0", "o1", "o2", "ons", "onc"]
 SIDES = ["k", "u0", "u1", "u2", "a", "b", "d", "la", "v2"]
 
 
-def kernel(dims, start_hbm, old_hbm, kappa_hbm, fine_hbm, ns_hbm, nc_hbm, padded, planes, sides,
+def kernel(dims, start_hbm, old_hbm, kappa_hbm, fine, following, coarse_next, padded, planes, sides,
            tiles, ztiles, zslots, yslots, xslots, send, recv, gsend, grecv, local):
     nt, ny, nz, rows, cols = dims
     chunk = rows // CHUNKS
@@ -228,19 +227,22 @@
         beside = beside(0 if c < CHUNKS // 2 else 1)
         return sweep(c * chunk, chunk, lambda r, acc: acc + quadratic(name, beside, weight, r), nothing)
 
+    spot = lax.broadcasted_iota(jnp.int32, (1, 128), 1)
+
     def lanes(acc):
         both = acc[:, 0:128]
         for i in range(1, cols // 128):
             both = both + acc[:, i * 128:(i + 1) * 128]
         return jnp.sum(both, axis=0, keepdims=True)
 
-    def burst(src, slots, base, devices, sem):
+    def burst(src, slots, devices, sem):
         for k, device in enumerate(devices):
             pltpu.make_async_remote_copy(
-                src_ref=src, dst_ref=slots.at[base + k], send_sem=gsend.at[sem], recv_sem=grecv.at[sem],
+                src_ref=src, dst_ref=slots.at[pl.ds(k, 1), :],
+                send_sem=gsend.at[sem], recv_sem=grecv.at[sem],
                 device_id=device, device_id_type=MESH,
             ).start()
-        whole = slots.at[pl.ds(base, len(devices))]
+        whole = slots.at[pl.ds(0, len(devices)), :]
         return pltpu.make_async_remote_copy(
             src_ref=whole, dst_ref=whole, send_sem=gsend.at[sem], recv_sem=grecv.at[sem],
             device_id=after, device_id_type=MESH,
@@ -249,40 +251,37 @@
     bursts = [shared]
 
     def reduce_z(n, accs):
-        accs = accs + [nothing] * (8 - len(accs))
-        tiles[n] = jnp.concatenate([lanes(acc) for acc in accs], axis=0)
-        waits = burst(tiles.at[n], zslots.at[n], 0, [z_peer(k) for k in range(1, nz)], 1 + 3 * n)
+        rows_of = jnp.concatenate([lanes(acc) for acc in accs + [nothing] * (8 - len(accs))], axis=0)
+        sums = jnp.sum(rows_of, axis=1, keepdims=True)
+        row = jnp.zeros((1, 128), jnp.float32)
+        for q in range(len(accs)):
+            row = jnp.where(spot == q, sums[q:q + 1, :], row)
+        tiles[n, 0:1, :] = row
+        devices = [z_peer(k) for k in range(1, nz)]
+        waits = burst(tiles.at[n, pl.ds(0, 1), :], zslots.at[n], devices, 1 + 3 * n)
         bursts.append(waits)
         return waits
 
     def reduce_y(n, waits, onward=False):
         waits.wait_recv()
-        total = tiles[n]
-        for k in range(nz - 1):
-            total = total + zslots[n, k]
-        ztiles[n] = total
-        out = [burst(ztiles.at[n], yslots.at[n], 0, [y_peer(k) for k in range(1, ny)], 2 + 3 * n)]
+        ztiles[n, 0:1, :] = tiles[n, 0:1, :] + jnp.sum(zslots[n, 0:nz - 1, :], axis=0, keepdims=True)
+        src = ztiles.at[n, pl.ds(0, 1), :]
+        out = [burst(src, yslots.at[n], [y_peer(k) for k in range(1, ny)], 2 + 3 * n)]
         if onward:
-            out.append(burst(ztiles.at[n], xslots, 0, [y_peer(k, next_t) for k in range(ny)], 3 + 3 * n))
+            out.append(burst(src, xslots, [y_peer(k, next_t) for k in range(ny)], 3 + 3 * n))
         bursts.extend(out)
         return out
 
     def total_own(n, waits):
         waits.wait_recv()
-        total = ztiles[n]
-        for k in range(ny - 1):
-            total = total + yslots[n, k]
-        return jnp.sum(total, axis=1, keepdims=True)
+        return ztiles[n, 0:1, :] + jnp.sum(yslots[n, 0:ny - 1, :], axis=0, keepdims=True)
 
     def total_last(waits):
         waits.wait_recv()
-        total = xslots[0]
-        for k in range(1, ny):
-            total = total + xslots[k]
-        return jnp.sum(total, axis=1, keepdims=True)
+        return jnp.sum(xslots[0:ny, :], axis=0, keepdims=True)
 
     def factors(sums, first, h):
-        s0, s1, s2, s3 = [sums[first + i:first + i + 1, :] for i in range(4)]
+        s0, s1, s2, s3 = [sums[:, first + i:first + i + 1] for i in range(4)]
         sigma = s1 / s0
         spread = jnp.maximum(s2 - s1 * sigma, 1e-30)
         bent = s3 - sigma * (s2 + s2) + sigma * sigma * s1
@@ -308,15 +307,16 @@
         plane["rc"][at(r), :] = rc
         return carry
 
-    a_in, b_in, d_in, la_in = [], [], [], []
-    for c in range(CHUNKS):
+    half = CHUNKS // 2
+    each = range(CHUNKS)
+    order = [i // 2 + (i % 2) * half for i in each]
+    a_in, b_in, d_in, la_in = {}, {}, {}, {}
+    for c in each:
         for j in range(3):
             arrive(u_in[c][j])
         sweep(c * chunk, chunk, first_fields, 0)
-        a_in.append(swap("a", c))
+        a_in[c] = swap("a", c)
     put_rc = put(plane["rc"], plane["xrc"], (next_t, me_y, me_z))
-    for c in range(CHUNKS):
-        b_in.append(swap("b", c))
 
     def first_heat(r, carry):
         s0, s1, s2 = carry
@@ -325,19 +325,20 @@
         return s0 + fold(mid * mid), s1 + fold(mid * out), s2 + fold(out * out)
 
     sums = (nothing,) * 3
-    for c in range(CHUNKS):
+    for c in each:
         arrive(a_in[c])
         sums = sweep(c * chunk, chunk, first_heat, sums)
-        la_in.append(swap("la", c))
-    d_in.append(swap("d", 0))
+        la_in[c] = swap("la", c)
+    b_in[0] = swap("b", 0)
 
     def second_field(r, carry):
         plane["lb"][at(r), :] = heat("b", r)[1]
         return carry
 
-    for c in range(CHUNKS):
-        arrive(b_in[c])
-        sweep(c * chunk, chunk, second_field, 0)
+    def take_b(chunks):
+        for c in chunks:
+            arrive(b_in[c])
+            sweep(c * chunk, chunk, second_field, 0)
 
     def second_heat(r, carry):
         mid, out = heat("la", r)
@@ -345,12 +346,14 @@
         return carry + fold(mid * out)
 
     s3 = nothing
-    for c in range(CHUNKS):
+    for c in each:
         arrive(la_in[c])
         s3 = sweep(c * chunk, chunk, second_heat, s3)
     z_wait = reduce_z(0, list(sums) + [s3])
-    for c in range(1, CHUNKS):
-        d_in.append(swap("d", c))
+    for c in each[1:]:
+        b_in[c] = swap("b", c)
+    for c in each[:2]:
+        d_in[c] = swap("d", c)
 
     def third_field(r, carry):
         s0, s1, s2 = carry
@@ -362,12 +365,16 @@
         return s0 + fold(rc * rc), s1 + fold(rc * vc), s2 + fold(vc * vc)
 
     coarse = (nothing,) * 3
-    arrive(d_in[0])
-    coarse = sweep(0, chunk, third_field, coarse)
+
+    def take_d(chunks, coarse):
+        for c in chunks:
+            arrive(d_in[c])
+            coarse = sweep(c * chunk, chunk, third_field, coarse)
+        return coarse
+
+    take_b(each[:4])
     (y_wait,) = reduce_y(0, z_wait)
-    if CHUNKS > 2:
-        arrive(d_in[1])
-        coarse = sweep(chunk, chunk, third_field, coarse)
+    take_b(each[4:])
     c0, c1 = factors(total_own(0, y_wait), 0, WIDTH[0])
 
     def second_node(r, carry):
@@ -375,7 +382,7 @@
         at_pad = pl.ds(PAD + r, BLOCK)
         a, la, lla = pad["a"][at_pad, :], pad["la"][at_pad, :], plane["lla"][at(r), :]
         move = c0 * a + c1 * la
-        plane["o0"][at(r), :] = pad["u0"][at_pad, :] + move
+        fine[0, at(r), :] = pad["u0"][at_pad, :] + move
         r2 = pad["b"][at_pad, :] + move
         v2 = plane["lb"][at(r), :] + c0 * la + c1 * lla
         plane["r2"][at(r), :] = r2
@@ -383,20 +390,13 @@
         return s0 + fold(r2 * r2), s1 + fold(r2 * v2), s2 + fold(v2 * v2)
 
     sums = (nothing,) * 3
-    v_in = {}
-    order = [i // 2 + (i % 2) * (CHUNKS // 2) for i in range(CHUNKS)]
+    v_in, w_in = {}, {}
     for c in order:
         sums = sweep(c * chunk, chunk, second_node, sums)
         v_in[c] = swap_half("v2", c, False)
-    w_in = {}
     for c in order[:2]:
         w_in[c] = swap_half("v2", c, True)
-    outs = [pltpu.make_async_copy(plane["o0"], fine_hbm.at[0], local.at[5])]
-    outs[0].start()
-    for c in range(2 if CHUNKS > 2 else 1, CHUNKS):
-        arrive(d_in[c])
-        coarse = sweep(c * chunk, chunk, third_field, coarse)
-    put_vc = put(inner("vc"), plane["xvc"], (next_t, me_y, me_z))
+    coarse = take_d(each[:2], coarse)
     s3 = nothing
     for c in order:
         arrive(v_in[c])
@@ -404,27 +404,30 @@
     z_wait = reduce_z(1, list(sums) + [s3])
     for c in order[2:]:
         w_in[c] = swap_half("v2", c, True)
-    vc_in = {c: give_half("vc", c) for c in order}
+    for c in each[2:]:
+        d_in[c] = swap("d", c)
 
     def third_heat(r, carry):
         plane["lv2"][at(r), :] = heat("v2", r)[1]
         return carry
 
-    for c in order[:2]:
-        arrive(w_in[c])
-        sweep(c * chunk, chunk, third_heat, 0)
+    def take_w(chunks):
+        for c in chunks:
+            arrive(w_in[c])
+            sweep(c * chunk, chunk, third_heat, 0)
+
+    take_w(order)
     (y_wait,) = reduce_y(1, z_wait)
-    for c in order[2:]:
-        arrive(w_in[c])
-        sweep(c * chunk, chunk, third_heat, 0)
+    coarse = take_d(each[2:5], coarse)
     e0, e1 = factors(total_own(1, y_wait), 0, WIDTH[1])
+    coarse = take_d(each[5:], coarse)
 
     def third_node(r, carry):
         s0, s1, s2 = carry
         at_pad = pl.ds(PAD + r, BLOCK)
         r2, v2, lv2 = plane["r2"][at(r), :], pad["v2"][at_pad, :], plane["lv2"][at(r), :]
         move = e0 * r2 + e1 * v2
-        plane["o1"][at(r), :] = pad["u1"][at_pad, :] + move
+        fine[1, at(r), :] = pad["u1"][at_pad, :] + move
         r3 = pad["d"][at_pad, :] + move
         v3 = plane["ld"][at(r), :] + e0 * v2 + e1 * lv2
         plane["r3"][at(r), :] = r3
@@ -432,14 +435,14 @@
         return s0 + fold(r3 * r3), s1 + fold(r3 * v3), s2 + fold(v3 * v3)
 
     sums = (nothing,) * 3
+    vc_in = {c: give_half("vc", c) for c in order}
+    put_vc = put(inner("vc"), plane["xvc"], (next_t, me_y, me_z))
     v3_in = {}
     for c in order:
         sums = sweep(c * chunk, chunk, third_node, sums)
         v3_in[c] = give_half("v3", c)
     put_r3 = put(plane["r3"], plane["xr3"], (next_t, me_y, me_z))
     put_v3 = put(inner("v3"), plane["xv3"], (next_t, me_y, me_z))
-    outs.append(pltpu.make_async_copy(plane["o1"], fine_hbm.at[1], local.at[6]))
-    outs[1].start()
     coarse3 = nothing
     for c in order:
         arrive(vc_in[c])
@@ -452,40 +455,34 @@
     y_wait, x_wait = reduce_y(2, z_wait, onward=True)
     for copy in (put_u, put_rc, put_vc, put_r3, put_v3):
         copy.wait_recv()
+    for copy in started:
+        copy.wait_send()
+    for waits in bursts[:-2]:
+        waits.wait_send()
     g0, g1 = factors(total_own(2, y_wait), 0, WIDTH[2])
 
     def last_node(r, carry):
         at_pad = pl.ds(PAD + r, BLOCK)
         move = g0 * plane["r3"][at(r), :] + g1 * pad["v3"][at_pad, :]
-        plane["o2"][at(r), :] = pad["u2"][at_pad, :] + move
+        fine[2, at(r), :] = pad["u2"][at_pad, :] + move
         return carry
 
     sweep(0, rows, last_node, 0)
-    outs.append(pltpu.make_async_copy(plane["o2"], fine_hbm.at[2], local.at[7]))
-    outs[2].start()
     sums = total_last(x_wait)
     p0, p1 = factors(sums, 0, WIDTH[2])
     q0, q1 = factors(sums, 4, STEP)
 
     def next_slice(r, carry):
         begin, guess = plane["s"][at(r), :], plane["xu"][at(r), :]
-        fine = guess + (p0 * plane["xr3"][at(r), :] + p1 * plane["xv3"][at(r), :])
-        coarse = guess + (q0 * plane["xrc"][at(r), :] + q1 * plane["xvc"][at(r), :])
-        plane["ons"][at(r), :] = jnp.where(me_t == 0, begin, fine)
-        plane["onc"][at(r), :] = jnp.where(me_t == 0, begin, coarse)
+        fine_end = guess + (p0 * plane["xr3"][at(r), :] + p1 * plane["xv3"][at(r), :])
+        coarse_end = guess + (q0 * plane["xrc"][at(r), :] + q1 * plane["xvc"][at(r), :])
+        following[at(r), :] = jnp.where(me_t == 0, begin, fine_end)
+        coarse_next[at(r), :] = jnp.where(me_t == 0, begin, coarse_end)
         return carry
 
     sweep(0, rows, next_slice, 0)
-    outs.append(pltpu.make_async_copy(plane["ons"], ns_hbm, local.at[8]))
-    outs.append(pltpu.make_async_copy(plane["onc"], nc_hbm, local.at[9]))
-    for copy in outs[3:]:
-        copy.start()
-    for copy in started:
-        copy.wait_send()
-    for waits in bursts:
+    for waits in bursts[-2:]:
         waits.wait_send()
-    for copy in outs:
-        copy.wait()
 
 
 def copies_needed():
@@ -495,31 +492,40 @@
 def on_device(dims, start_value, old_nodes, diffusivity):
     nt, ny, nz, rows, cols = dims
     anywhere = pl.BlockSpec(memory_space=pl.ANY)
+    near = pl.BlockSpec(memory_space=pltpu.VMEM)
     plane = jax.ShapeDtypeStruct((rows, cols), jnp.float32)
+    inputs = [
+        pltpu.with_memory_space_constraint(value, pltpu.MemorySpace.HBM)
+        for value in (
+            start_value.reshape(rows, cols),
+            old_nodes.reshape(3, rows, cols),
+            diffusivity.reshape(rows, cols),
+        )
+    ]
     fine, following, coarse = pl.pallas_call(
         functools.partial(kernel, dims),
         out_shape=(jax.ShapeDtypeStruct((3, rows, cols), jnp.float32), plane, plane),
         in_specs=[anywhere] * 3,
-        out_specs=(anywhere,) * 3,
+        out_specs=(near,) * 3,
         scratch_shapes=[
             pltpu.VMEM((len(PADDED), rows + 2 * PAD, cols), jnp.float32),
             pltpu.VMEM((len(PLANES), rows, cols), jnp.float32),
             pltpu.VMEM((len(SIDES), 2, rows, cols), jnp.float32),
             pltpu.VMEM((3, 8, 128), jnp.float32),
             pltpu.VMEM((3, 8, 128), jnp.float32),
-            pltpu.VMEM((3, nz - 1, 8, 128), jnp.float32),
-            pltpu.VMEM((3, ny - 1, 8, 128), jnp.float32),
-            pltpu.VMEM((ny, 8, 128), jnp.float32),
+            pltpu.VMEM((3, 16, 128), jnp.float32),
+            pltpu.VMEM((3, 8, 128), jnp.float32),
+            pltpu.VMEM((8, 128), jnp.float32),
             pltpu.SemaphoreType.DMA((copies_needed(),)),
             pltpu.SemaphoreType.DMA((copies_needed(),)),
             pltpu.SemaphoreType.DMA((10,)),
             pltpu.SemaphoreType.DMA((10,)),
-            pltpu.SemaphoreType.DMA((10,)),
+            pltpu.SemaphoreType.DMA((5,)),
         ],
         compiler_params=pltpu.CompilerParams(
-            collective_id=0, has_side_effects=True, vmem_limit_bytes=60 * 1024 * 1024
+            collective_id=0, has_side_effects=True, vmem_limit_bytes=40 * 1024 * 1024
         ),
-    )(start_value.reshape(rows, cols), old_nodes.reshape(3, rows, cols), diffusivity.reshape(rows, cols))
+    )(*inputs)
     return (
         fine.reshape(1, 3, 1, rows, cols),
         following.reshape(1, 1, rows, cols),

time: 160 us -> 151 us (0.944)
  the two profiles are of different devices: /device:TPU:6 before, /device:TPU:1 now
where the time goes in v2:
time: 151 us; the launch traced here: 150 us
  Pallas kernels  146 us (97%)
  local copies, waits for them, and re-layouts  2.73 us (2%)
    pallas_call x1, Pallas kernels, on_device(): pl.pallas_call(functools.partial(kernel, dims), out_shape=(jax.ShapeDtype...  146 us

profile of v2, /device:TPU:1, one launch (start us, length us, event | category | flops | bytes accessed | tf_op | source)
XLA Modules:
  0.0 149.7 jit_solution(3898477596762492724)
XLA Ops:
  0.6 146.3 %shard_map.58 = (f32[3,512,256]{2,1,0:T(8,128)S(1)}, f32[512,256]{1,0:T(8,128)S(1)}, f32[512,256]{1,0:T(8,128)S(1)}) custom-call(f32[512,256]{1,0:T(8,128)} %bitcast.12, f32[3,512,256]{2,1,0:T(8,128)} %bitcast.11, f32[512,256]{1,0:T(8,128)} %bitcast.13), custom_call_target="tpu_custom_call" | custom-call | tf_op jit(solution)/shard_map/pallas_call | solution.py:505
  147.0 1.1 copy.10
  148.1 0.8 copy.11
  148.9 0.8 copy.12

commit v3 on v2

--- a/solution.py
+++ b/solution.py
@@ -46,6 +46,9 @@
            tiles, ztiles, zslots, yslots, xslots, send, recv, gsend, grecv, local):
     nt, ny, nz, rows, cols = dims
     chunk = rows // CHUNKS
+    half = CHUNKS // 2
+    each = range(CHUNKS)
+    order = [i // 2 + (i % 2) * half for i in each]
     me_t, me_y, me_z = lax.axis_index("tm"), lax.axis_index("y"), lax.axis_index("z")
     place = me_y * nz + me_z
     slabs = ny * nz
@@ -95,51 +98,67 @@
         copy.wait()
     pl.semaphore_wait(barrier, len(greeted))
 
-    started = []
-
-    def put(src, dst, device):
-        i = len(started)
-        copy = pltpu.make_async_remote_copy(
-            src_ref=src, dst_ref=dst, send_sem=send.at[i], recv_sem=recv.at[i],
+    taken = []
+
+    def put(src, dst, device, group, slot):
+        pltpu.make_async_remote_copy(
+            src_ref=src, dst_ref=dst, send_sem=send.at[group], recv_sem=recv.at[slot],
             device_id=device, device_id_type=MESH,
+        ).start()
+
+    def expect(region, group, slot):
+        return pltpu.make_async_remote_copy(
+            src_ref=region, dst_ref=region, send_sem=send.at[group], recv_sem=recv.at[slot],
+            device_id=after, device_id_type=MESH,
         )
-        copy.start()
-        started.append(copy)
-        return copy
+
+    def fresh_slot():
+        taken.append(0)
+        return len(taken) - 1
+
+    def swap_all(names, c):
+        slot = fresh_slot()
+        there = pl.ds(c * chunk, chunk)
+        for name in names:
+            here = inner(name, c * chunk, chunk)
+            put(here, side[name].at[0, there, :], after, 0, slot)
+            put(here, side[name].at[1, there, :], before, 0, slot)
+        first = SIDES.index(names[0])
+        return expect(sides.at[pl.ds(first, len(names)), :, there, :], 0, slot)
 
     def swap(name, c):
-        here = inner(name, c * chunk, chunk)
-        there = pl.ds(c * chunk, chunk)
-        return [
-            put(here, side[name].at[0, there, :], after),
-            put(here, side[name].at[1, there, :], before),
-        ]
-
-    def swap_half(name, c, second):
-        here = inner(name, c * chunk, chunk)
-        there = pl.ds(c * chunk, chunk)
-        up = (c < CHUNKS // 2) != second
-        return [put(here, side[name].at[0 if up else 1, there, :], after if up else before)]
-
-    def give_half(name, c):
-        up = c < CHUNKS // 2
-        here = inner(name, c * chunk, chunk)
-        there = plane["h" + name].at[pl.ds(c * chunk, chunk), :]
-        return [put(here, there, after if up else before)]
-
-    def arrive(batch):
-        for copy in batch:
-            copy.wait_recv()
+        return swap_all([name], c)
+
+    def swap_half(name, i, second):
+        slot = fresh_slot()
+        for c, up in ((i, not second), (i + half, second)):
+            there = pl.ds(c * chunk, chunk)
+            dst = side[name].at[0 if up else 1, there, :]
+            put(inner(name, c * chunk, chunk), dst, after if up else before, 0, slot)
+        return expect(side[name].at[:, pl.ds(0, chunk), :], 0, slot)
+
+    def give_half(name, i):
+        slot = fresh_slot()
+        for c, up in ((i, True), (i + half, False)):
+            dst = plane["h" + name].at[pl.ds(c * chunk, chunk), :]
+            put(inner(name, c * chunk, chunk), dst, after if up else before, 1, slot)
+        return expect(side["v2"].at[:, pl.ds(0, chunk), :], 1, slot)
+
+    def arrive(waiter):
+        waiter.wait_recv()
 
     share = rows // nt
     own = pl.multiple_of(me_t * share, share)
     mine = pl.ds(own, share)
     k_src = pad["k"].at[pl.ds(pl.multiple_of(PAD + own, PAD), share), :]
-    k_in = [put(k_src, side["k"].at[0, mine, :], after), put(k_src, side["k"].at[1, mine, :], before)]
-    u_in = []
-    for c in range(CHUNKS):
-        u_in.append([swap("u%d" % j, c) for j in range(3)])
-    put_u = put(inner("u2"), plane["xu"], (next_t, me_y, me_z))
+    k_slot = fresh_slot()
+    put(k_src, side["k"].at[0, mine, :], after, 3, k_slot)
+    put(k_src, side["k"].at[1, mine, :], before, 3, k_slot)
+    k_in = expect(side["k"].at[:, mine, :], 3, k_slot)
+    u_in = [swap_all(["u0", "u1", "u2"], c) for c in range(CHUNKS)]
+    next_device = (next_t, me_y, me_z)
+    early, late = fresh_slot(), fresh_slot()
+    put(inner("u2"), plane["xu"], next_device, 2, early)
     arrive(k_in)
     for s in range(2):
         block = side["k"].at[s, mine, :]
@@ -293,6 +312,9 @@
         c0 = one + two * slope - c1 * sigma
         return c0, c1
 
+    def whole(x):
+        return jnp.concatenate([jnp.broadcast_to(x, (8, cols))] * (BLOCK // 8), axis=0)
+
     def first_fields(r, carry):
         mids, images = zip(*[heat("u%d" % j, r) for j in range(3)])
         begin = plane["s"][at(r), :]
@@ -307,16 +329,12 @@
         plane["rc"][at(r), :] = rc
         return carry
 
-    half = CHUNKS // 2
-    each = range(CHUNKS)
-    order = [i // 2 + (i % 2) * half for i in each]
     a_in, b_in, d_in, la_in = {}, {}, {}, {}
     for c in each:
-        for j in range(3):
-            arrive(u_in[c][j])
+        arrive(u_in[c])
         sweep(c * chunk, chunk, first_fields, 0)
         a_in[c] = swap("a", c)
-    put_rc = put(plane["rc"], plane["xrc"], (next_t, me_y, me_z))
+    put(plane["rc"], plane["xrc"], next_device, 2, early)
 
     def first_heat(r, carry):
         s0, s1, s2 = carry
@@ -352,7 +370,7 @@
     z_wait = reduce_z(0, list(sums) + [s3])
     for c in each[1:]:
         b_in[c] = swap("b", c)
-    for c in each[:2]:
+    for c in order[:2]:
         d_in[c] = swap("d", c)
 
     def third_field(r, carry):
@@ -365,17 +383,20 @@
         return s0 + fold(rc * rc), s1 + fold(rc * vc), s2 + fold(vc * vc)
 
     coarse = (nothing,) * 3
+    vc_in = {}
 
     def take_d(chunks, coarse):
         for c in chunks:
             arrive(d_in[c])
             coarse = sweep(c * chunk, chunk, third_field, coarse)
+            if c >= half:
+                vc_in[c - half] = give_half("vc", c - half)
         return coarse
 
     take_b(each[:4])
     (y_wait,) = reduce_y(0, z_wait)
     take_b(each[4:])
-    c0, c1 = factors(total_own(0, y_wait), 0, WIDTH[0])
+    c0, c1 = [whole(x) for x in factors(total_own(0, y_wait), 0, WIDTH[0])]
 
     def second_node(r, carry):
         s0, s1, s2 = carry
@@ -393,34 +414,36 @@
     v_in, w_in = {}, {}
     for c in order:
         sums = sweep(c * chunk, chunk, second_node, sums)
-        v_in[c] = swap_half("v2", c, False)
-    for c in order[:2]:
-        w_in[c] = swap_half("v2", c, True)
-    coarse = take_d(each[:2], coarse)
+        if c >= half:
+            v_in[c - half] = swap_half("v2", c - half, False)
+    w_in[0] = swap_half("v2", 0, True)
     s3 = nothing
-    for c in order:
-        arrive(v_in[c])
-        s3 = s3 + moments("v2", lambda s: side["v2"].at[s], c)
+    for i in range(half):
+        arrive(v_in[i])
+        for c in (i, i + half):
+            s3 = s3 + moments("v2", lambda s: side["v2"].at[s], c)
     z_wait = reduce_z(1, list(sums) + [s3])
+    for i in range(1, half):
+        w_in[i] = swap_half("v2", i, True)
     for c in order[2:]:
-        w_in[c] = swap_half("v2", c, True)
-    for c in each[2:]:
         d_in[c] = swap("d", c)
 
     def third_heat(r, carry):
         plane["lv2"][at(r), :] = heat("v2", r)[1]
         return carry
 
-    def take_w(chunks):
-        for c in chunks:
-            arrive(w_in[c])
-            sweep(c * chunk, chunk, third_heat, 0)
-
-    take_w(order)
+    def take_w(pairs):
+        for i in pairs:
+            arrive(w_in[i])
+            for c in (i, i + half):
+                sweep(c * chunk, chunk, third_heat, 0)
+
+    take_w(range(2))
     (y_wait,) = reduce_y(1, z_wait)
-    coarse = take_d(each[2:5], coarse)
-    e0, e1 = factors(total_own(1, y_wait), 0, WIDTH[1])
-    coarse = take_d(each[5:], coarse)
+    take_w(range(2, half))
+    coarse = take_d(order[:5], coarse)
+    e0, e1 = [whole(x) for x in factors(total_own(1, y_wait), 0, WIDTH[1])]
+    coarse = take_d(order[5:], coarse)
 
     def third_node(r, carry):
         s0, s1, s2 = carry
@@ -435,31 +458,41 @@
         return s0 + fold(r3 * r3), s1 + fold(r3 * v3), s2 + fold(v3 * v3)
 
     sums = (nothing,) * 3
-    vc_in = {c: give_half("vc", c) for c in order}
-    put_vc = put(inner("vc"), plane["xvc"], (next_t, me_y, me_z))
+    put(inner("vc"), plane["xvc"], next_device, 2, early)
     v3_in = {}
     for c in order:
         sums = sweep(c * chunk, chunk, third_node, sums)
-        v3_in[c] = give_half("v3", c)
-    put_r3 = put(plane["r3"], plane["xr3"], (next_t, me_y, me_z))
-    put_v3 = put(inner("v3"), plane["xv3"], (next_t, me_y, me_z))
+        if c >= half:
+            v3_in[c - half] = give_half("v3", c - half)
+    put(plane["r3"], plane["xr3"], next_device, 2, late)
+    put(inner("v3"), plane["xv3"], next_device, 2, late)
     coarse3 = nothing
-    for c in order:
-        arrive(vc_in[c])
-        coarse3 = coarse3 + moments("vc", lambda s: plane["hvc"], c)
+    for i in range(half):
+        arrive(vc_in[i])
+        for c in (i, i + half):
+            coarse3 = coarse3 + moments("vc", lambda s: plane["hvc"], c)
     s3 = nothing
-    for c in order:
-        arrive(v3_in[c])
-        s3 = s3 + moments("v3", lambda s: plane["hv3"], c)
+    for i in range(half):
+        arrive(v3_in[i])
+        for c in (i, i + half):
+            s3 = s3 + moments("v3", lambda s: plane["hv3"], c)
     z_wait = reduce_z(2, list(sums) + [s3] + list(coarse) + [coarse3])
+    expect(planes.at[pl.ds(0, 3)], 2, early).wait_recv()
+
+    def first_slice(r, carry):
+        plane["xu"][at(r), :] = jnp.where(me_t == 0, plane["s"][at(r), :], plane["xu"][at(r), :])
+        return carry
+
+    sweep(0, rows, first_slice, 0)
     y_wait, x_wait = reduce_y(2, z_wait, onward=True)
-    for copy in (put_u, put_rc, put_vc, put_r3, put_v3):
-        copy.wait_recv()
-    for copy in started:
-        copy.wait_send()
+    expect(planes.at[pl.ds(0, 2)], 2, late).wait_recv()
+    expect(sides.at[pl.ds(1, len(SIDES) - 1)], 0, 0).wait_send()
+    expect(planes.at[pl.ds(0, 2)], 1, 0).wait_send()
+    expect(planes.at[pl.ds(0, 5)], 2, 0).wait_send()
+    k_in.wait_send()
     for waits in bursts[:-2]:
         waits.wait_send()
-    g0, g1 = factors(total_own(2, y_wait), 0, WIDTH[2])
+    g0, g1 = [whole(x) for x in factors(total_own(2, y_wait), 0, WIDTH[2])]
 
     def last_node(r, carry):
         at_pad = pl.ds(PAD + r, BLOCK)
@@ -469,15 +502,13 @@
 
     sweep(0, rows, last_node, 0)
     sums = total_last(x_wait)
-    p0, p1 = factors(sums, 0, WIDTH[2])
-    q0, q1 = factors(sums, 4, STEP)
+    passed = [jnp.where(me_t == 0, 0.0, x) for x in factors(sums, 0, WIDTH[2]) + factors(sums, 4, STEP)]
+    p0, p1, q0, q1 = [whole(x) for x in passed]
 
     def next_slice(r, carry):
-        begin, guess = plane["s"][at(r), :], plane["xu"][at(r), :]
-        fine_end = guess + (p0 * plane["xr3"][at(r), :] + p1 * plane["xv3"][at(r), :])
-        coarse_end = guess + (q0 * plane["xrc"][at(r), :] + q1 * plane["xvc"][at(r), :])
-        following[at(r), :] = jnp.where(me_t == 0, begin, fine_end)
-        coarse_next[at(r), :] = jnp.where(me_t == 0, begin, coarse_end)
+        guess = plane["xu"][at(r), :]
+        following[at(r), :] = guess + (p0 * plane["xr3"][at(r), :] + p1 * plane["xv3"][at(r), :])
+        coarse_next[at(r), :] = guess + (q0 * plane["xrc"][at(r), :] + q1 * plane["xvc"][at(r), :])
         return carry
 
     sweep(0, rows, next_slice, 0)
@@ -485,8 +516,21 @@
         waits.wait_send()
 
 
-def copies_needed():
-    return 2 + 6 * CHUNKS + 5 * 2 * CHUNKS + 2 * CHUNKS + 5
+def slots_needed():
+    return 1 + 2 + 5 * CHUNKS + 4 * (CHUNKS // 2)
+
+
+def leave(fine, following, coarse, fine_hbm, following_hbm, coarse_hbm, sem):
+    copies = [
+        pltpu.make_async_copy(src, dst, sem.at[i])
+        for i, (src, dst) in enumerate(
+            [(fine, fine_hbm), (following, following_hbm), (coarse, coarse_hbm)]
+        )
+    ]
+    for copy in copies:
+        copy.start()
+    for copy in copies:
+        copy.wait()
 
 
 def on_device(dims, start_value, old_nodes, diffusivity):
@@ -516,8 +560,8 @@
             pltpu.VMEM((3, 16, 128), jnp.float32),
             pltpu.VMEM((3, 8, 128), jnp.float32),
             pltpu.VMEM((8, 128), jnp.float32),
-            pltpu.SemaphoreType.DMA((copies_needed(),)),
-            pltpu.SemaphoreType.DMA((copies_needed(),)),
+            pltpu.SemaphoreType.DMA((4,)),
+            pltpu.SemaphoreType.DMA((slots_needed(),)),
             pltpu.SemaphoreType.DMA((10,)),
             pltpu.SemaphoreType.DMA((10,)),
             pltpu.SemaphoreType.DMA((5,)),
@@ -526,6 +570,14 @@
             collective_id=0, has_side_effects=True, vmem_limit_bytes=40 * 1024 * 1024
         ),
     )(*inputs)
+    fine, following, coarse = pl.pallas_call(
+        leave,
+        out_shape=(jax.ShapeDtypeStruct((3, rows, cols), jnp.float32), plane, plane),
+        in_specs=[anywhere] * 3,
+        out_specs=(anywhere,) * 3,
+        scratch_shapes=[pltpu.SemaphoreType.DMA((3,))],
+        compiler_params=pltpu.CompilerParams(vmem_limit_bytes=40 * 1024 * 1024),
+    )(fine, following, coarse)
     return (
         fine.reshape(1, 3, 1, rows, cols),
         following.reshape(1, 1, rows, cols),

time: 151 us -> 143 us (0.947)
  Pallas kernels: 146 us -> 142 us
  local copies, waits for them, and re-layouts: 2.73 us -> 0 us
    pallas_call x1, Pallas kernels: 146 us -> 140 us  [on_device(): pl.pallas_call(functools.partial(kernel, dims), out_shape=(jax.ShapeDtype...]
    unnamed x3 -> x0, local copies, waits for them, and re-layouts: 2.73 us -> none
    pallas_call x0 -> x1, Pallas kernels: none -> 1.51 us  [on_device(): pl.pallas_call(leave, out_shape=(jax.ShapeDtypeStruct((3, rows, cols), jn...]
where the time goes in v3:
time: 143 us
  Pallas kernels  142 us (99%)
    pallas_call x1, Pallas kernels, on_device(): pl.pallas_call(functools.partial(kernel, dims), out_shape=(jax.ShapeDtype...  140 us

profile of v3, /device:TPU:1, one launch (start us, length us, event | category | flops | bytes accessed | tf_op | source)
XLA Modules:
  0.0 142.6 jit_solution(16107305093825764517)
XLA Ops:
  0.6 140.4 %shard_map.58 = (f32[3,512,256]{2,1,0:T(8,128)S(1)}, f32[512,256]{1,0:T(8,128)S(1)}, f32[512,256]{1,0:T(8,128)S(1)}) custom-call(f32[512,256]{1,0:T(8,128)} %bitcast.9, f32[3,512,256]{2,1,0:T(8,128)} %bitcast.8, f32[512,256]{1,0:T(8,128)} %bitcast.10), custom_call_target="tpu_custom_call" | custom-call | tf_op jit(solution)/shard_map/pallas_call | solution.py:549
  141.1 1.5 %shard_map.59 = (f32[3,512,256]{2,1,0:T(8,128)}, f32[512,256]{1,0:T(8,128)}, f32[512,256]{1,0:T(8,128)}) custom-call(f32[3,512,256]{2,1,0:T(8,128)S(1)} %get-tuple-element.9.fine, f32[512,256]{1,0:T(8,128)S(1)} %get-tuple-element.10.following, f32[512,256]{1,0:T(8,128)S(1)} %get-tuple-element.11.coarse), custom_call_target="tpu_custom_call" | custom-call | tf_op jit(solution)/shard_map/pallas_call | solution.py:573

commit v4 on v3

--- a/solution.py
+++ b/solution.py
@@ -144,6 +144,12 @@
             put(inner(name, c * chunk, chunk), dst, after if up else before, 1, slot)
         return expect(side["v2"].at[:, pl.ds(0, chunk), :], 1, slot)
 
+    next_device = (next_t, me_y, me_z)
+    early, late = fresh_slot(), fresh_slot()
+
+    def onward(src, name, c, slot):
+        put(src, plane[name].at[pl.ds(c * chunk, chunk), :], next_device, 2, slot)
+
     def arrive(waiter):
         waiter.wait_recv()
 
@@ -156,8 +162,6 @@
     put(k_src, side["k"].at[1, mine, :], before, 3, k_slot)
     k_in = expect(side["k"].at[:, mine, :], 3, k_slot)
     u_in = [swap_all(["u0", "u1", "u2"], c) for c in range(CHUNKS)]
-    next_device = (next_t, me_y, me_z)
-    early, late = fresh_slot(), fresh_slot()
     put(inner("u2"), plane["xu"], next_device, 2, early)
     arrive(k_in)
     for s in range(2):
@@ -281,12 +285,12 @@
         bursts.append(waits)
         return waits
 
-    def reduce_y(n, waits, onward=False):
+    def reduce_y(n, waits, also=False):
         waits.wait_recv()
         ztiles[n, 0:1, :] = tiles[n, 0:1, :] + jnp.sum(zslots[n, 0:nz - 1, :], axis=0, keepdims=True)
         src = ztiles.at[n, pl.ds(0, 1), :]
         out = [burst(src, yslots.at[n], [y_peer(k) for k in range(1, ny)], 2 + 3 * n)]
-        if onward:
+        if also:
             out.append(burst(src, xslots, [y_peer(k, next_t) for k in range(ny)], 3 + 3 * n))
         bursts.extend(out)
         return out
@@ -347,7 +351,8 @@
         arrive(a_in[c])
         sums = sweep(c * chunk, chunk, first_heat, sums)
         la_in[c] = swap("la", c)
-    b_in[0] = swap("b", 0)
+    for c in each[:3]:
+        b_in[c] = swap("b", c)
 
     def second_field(r, carry):
         plane["lb"][at(r), :] = heat("b", r)[1]
@@ -368,9 +373,9 @@
         arrive(la_in[c])
         s3 = sweep(c * chunk, chunk, second_heat, s3)
     z_wait = reduce_z(0, list(sums) + [s3])
-    for c in each[1:]:
+    for c in each[3:]:
         b_in[c] = swap("b", c)
-    for c in order[:2]:
+    for c in order[:4]:
         d_in[c] = swap("d", c)
 
     def third_field(r, carry):
@@ -389,6 +394,7 @@
         for c in chunks:
             arrive(d_in[c])
             coarse = sweep(c * chunk, chunk, third_field, coarse)
+            onward(inner("vc", c * chunk, chunk), "xvc", c, early)
             if c >= half:
                 vc_in[c - half] = give_half("vc", c - half)
         return coarse
@@ -416,16 +422,16 @@
         sums = sweep(c * chunk, chunk, second_node, sums)
         if c >= half:
             v_in[c - half] = swap_half("v2", c - half, False)
-    w_in[0] = swap_half("v2", 0, True)
+    coarse = take_d(order[:4], coarse)
     s3 = nothing
     for i in range(half):
         arrive(v_in[i])
         for c in (i, i + half):
             s3 = s3 + moments("v2", lambda s: side["v2"].at[s], c)
     z_wait = reduce_z(1, list(sums) + [s3])
-    for i in range(1, half):
+    for i in range(half):
         w_in[i] = swap_half("v2", i, True)
-    for c in order[2:]:
+    for c in order[4:]:
         d_in[c] = swap("d", c)
 
     def third_heat(r, carry):
@@ -441,9 +447,9 @@
     take_w(range(2))
     (y_wait,) = reduce_y(1, z_wait)
     take_w(range(2, half))
-    coarse = take_d(order[:5], coarse)
+    coarse = take_d(order[4:6], coarse)
     e0, e1 = [whole(x) for x in factors(total_own(1, y_wait), 0, WIDTH[1])]
-    coarse = take_d(order[5:], coarse)
+    coarse = take_d(order[6:], coarse)
 
     def third_node(r, carry):
         s0, s1, s2 = carry
@@ -458,14 +464,13 @@
         return s0 + fold(r3 * r3), s1 + fold(r3 * v3), s2 + fold(v3 * v3)
 
     sums = (nothing,) * 3
-    put(inner("vc"), plane["xvc"], next_device, 2, early)
     v3_in = {}
     for c in order:
         sums = sweep(c * chunk, chunk, third_node, sums)
         if c >= half:
             v3_in[c - half] = give_half("v3", c - half)
-    put(plane["r3"], plane["xr3"], next_device, 2, late)
-    put(inner("v3"), plane["xv3"], next_device, 2, late)
+        onward(plane["r3"].at[pl.ds(c * chunk, chunk), :], "xr3", c, late)
+        onward(inner("v3", c * chunk, chunk), "xv3", c, late)
     coarse3 = nothing
     for i in range(half):
         arrive(vc_in[i])
@@ -484,7 +489,7 @@
         return carry
 
     sweep(0, rows, first_slice, 0)
-    y_wait, x_wait = reduce_y(2, z_wait, onward=True)
+    y_wait, x_wait = reduce_y(2, z_wait, also=True)
     expect(planes.at[pl.ds(0, 2)], 2, late).wait_recv()
     expect(sides.at[pl.ds(1, len(SIDES) - 1)], 0, 0).wait_send()
     expect(planes.at[pl.ds(0, 2)], 1, 0).wait_send()

time: 143 us -> 139 us (0.972)
  Pallas kernels: 142 us -> 138 us
    pallas_call x1, Pallas kernels: 140 us -> 137 us  [on_device(): pl.pallas_call(functools.partial(kernel, dims), out_shape=(jax.ShapeDtype...]
where the time goes in v4:
time: 139 us
  Pallas kernels  138 us (99%)
    pallas_call x1, Pallas kernels, on_device(): pl.pallas_call(functools.partial(kernel, dims), out_shape=(jax.ShapeDtype...  137 us

profile of v4, /device:TPU:1, one launch (start us, length us, event | category | flops | bytes accessed | tf_op | source)
XLA Modules:
  0.0 138.7 jit_solution(1811727320636194136)
XLA Ops:
  0.6 136.5 %shard_map.58 = (f32[3,512,256]{2,1,0:T(8,128)S(1)}, f32[512,256]{1,0:T(8,128)S(1)}, f32[512,256]{1,0:T(8,128)S(1)}) custom-call(f32[512,256]{1,0:T(8,128)} %bitcast.9, f32[3,512,256]{2,1,0:T(8,128)} %bitcast.8, f32[512,256]{1,0:T(8,128)} %bitcast.10), custom_call_target="tpu_custom_call" | custom-call | tf_op jit(solution)/shard_map/pallas_call | solution.py:554
  137.2 1.5 %shard_map.59 = (f32[3,512,256]{2,1,0:T(8,128)}, f32[512,256]{1,0:T(8,128)}, f32[512,256]{1,0:T(8,128)}) custom-call(f32[3,512,256]{2,1,0:T(8,128)S(1)} %get-tuple-element.9.fine, f32[512,256]{1,0:T(8,128)S(1)} %get-tuple-element.10.following, f32[512,256]{1,0:T(8,128)S(1)} %get-tuple-element.11.coarse), custom_call_target="tpu_custom_call" | custom-call | tf_op jit(solution)/shard_map/pallas_call | solution.py:578

commit v5 on v4

--- a/solution.py
+++ b/solution.py
@@ -259,11 +259,12 @@
         return jnp.sum(both, axis=0, keepdims=True)
 
     def burst(src, slots, devices, sem):
-        for k, device in enumerate(devices):
+        middle = (len(devices) - 1) / 2
+        for k in sorted(range(len(devices)), key=lambda k: abs(k - middle)):
             pltpu.make_async_remote_copy(
                 src_ref=src, dst_ref=slots.at[pl.ds(k, 1), :],
                 send_sem=gsend.at[sem], recv_sem=grecv.at[sem],
-                device_id=device, device_id_type=MESH,
+                device_id=devices[k], device_id_type=MESH,
             ).start()
         whole = slots.at[pl.ds(0, len(devices)), :]
         return pltpu.make_async_remote_copy(
@@ -423,13 +424,14 @@
         if c >= half:
             v_in[c - half] = swap_half("v2", c - half, False)
     coarse = take_d(order[:4], coarse)
+    w_in[0] = swap_half("v2", 0, True)
     s3 = nothing
     for i in range(half):
         arrive(v_in[i])
         for c in (i, i + half):
             s3 = s3 + moments("v2", lambda s: side["v2"].at[s], c)
     z_wait = reduce_z(1, list(sums) + [s3])
-    for i in range(half):
+    for i in range(1, half):
         w_in[i] = swap_half("v2", i, True)
     for c in order[4:]:
         d_in[c] = swap("d", c)
@@ -449,7 +451,6 @@
     take_w(range(2, half))
     coarse = take_d(order[4:6], coarse)
     e0, e1 = [whole(x) for x in factors(total_own(1, y_wait), 0, WIDTH[1])]
-    coarse = take_d(order[6:], coarse)
 
     def third_node(r, carry):
         s0, s1, s2 = carry
@@ -465,18 +466,24 @@
 
     sums = (nothing,) * 3
     v3_in = {}
-    for c in order:
-        sums = sweep(c * chunk, chunk, third_node, sums)
-        if c >= half:
-            v3_in[c - half] = give_half("v3", c - half)
-        onward(plane["r3"].at[pl.ds(c * chunk, chunk), :], "xr3", c, late)
-        onward(inner("v3", c * chunk, chunk), "xv3", c, late)
-    coarse3 = nothing
+
+    def take_node(chunks, sums):
+        for c in chunks:
+            sums = sweep(c * chunk, chunk, third_node, sums)
+            if c >= half:
+                v3_in[c - half] = give_half("v3", c - half)
+            onward(plane["r3"].at[pl.ds(c * chunk, chunk), :], "xr3", c, late)
+            onward(inner("v3", c * chunk, chunk), "xv3", c, late)
+        return sums
+
+    sums = take_node(order[:4], sums)
+    coarse = take_d(order[6:], coarse)
+    sums = take_node(order[4:], sums)
+    coarse3, s3 = nothing, nothing
     for i in range(half):
         arrive(vc_in[i])
         for c in (i, i + half):
             coarse3 = coarse3 + moments("vc", lambda s: plane["hvc"], c)
-    s3 = nothing
     for i in range(half):
         arrive(v3_in[i])
         for c in (i, i + half):

time: 139 us -> 139 us (level)
  no operation moved by 1% of the time
where the time goes in v5:
time: 139 us; the launch traced here: 138 us
  Pallas kernels  138 us (99%)
    pallas_call x1, Pallas kernels, on_device(): pl.pallas_call(functools.partial(kernel, dims), out_shape=(jax.ShapeDtype...  136 us

profile of v5, /device:TPU:1, one launch (start us, length us, event | category | flops | bytes accessed | tf_op | source)
XLA Modules:
  0.0 138.4 jit_solution(14840286934741600961)
XLA Ops:
  0.6 136.3 %shard_map.58 = (f32[3,512,256]{2,1,0:T(8,128)S(1)}, f32[512,256]{1,0:T(8,128)S(1)}, f32[512,256]{1,0:T(8,128)S(1)}) custom-call(f32[512,256]{1,0:T(8,128)} %bitcast.9, f32[3,512,256]{2,1,0:T(8,128)} %bitcast.8, f32[512,256]{1,0:T(8,128)} %bitcast.10), custom_call_target="tpu_custom_call" | custom-call | tf_op jit(solution)/shard_map/pallas_call | solution.py:561
  136.9 1.5 %shard_map.59 = (f32[3,512,256]{2,1,0:T(8,128)}, f32[512,256]{1,0:T(8,128)}, f32[512,256]{1,0:T(8,128)}) custom-call(f32[3,512,256]{2,1,0:T(8,128)S(1)} %get-tuple-element.9.fine, f32[512,256]{1,0:T(8,128)S(1)} %get-tuple-element.10.following, f32[512,256]{1,0:T(8,128)S(1)} %get-tuple-element.11.coarse), custom_call_target="tpu_custom_call" | custom-call | tf_op jit(solution)/shard_map/pallas_call | solution.py:585

commit v6 on v5

--- a/solution.py
+++ b/solution.py
@@ -90,12 +90,6 @@
     greeted += [y_peer(k, last_t) for k in range(ny)]
     for device in greeted:
         pl.semaphore_signal(barrier, inc=1, device_id=device, device_id_type=MESH)
-    edge = jnp.zeros((PAD, cols), jnp.float32)
-    for name in PADDED:
-        pad[name][pl.ds(0, PAD), :] = edge
-        pad[name][pl.ds(PAD + rows, PAD), :] = edge
-    for copy in copies:
-        copy.wait()
     pl.semaphore_wait(barrier, len(greeted))
 
     taken = []
@@ -153,30 +147,53 @@
     def arrive(waiter):
         waiter.wait_recv()
 
-    share = rows // nt
-    own = pl.multiple_of(me_t * share, share)
+    givers = nt // 2
+    share = rows // givers
+    own = pl.multiple_of(lax.div(me_t, 2) * share, share)
     mine = pl.ds(own, share)
-    k_src = pad["k"].at[pl.ds(pl.multiple_of(PAD + own, PAD), share), :]
+    gives = lax.rem(me_t, 2) == 1
     k_slot = fresh_slot()
-    put(k_src, side["k"].at[0, mine, :], after, 3, k_slot)
-    put(k_src, side["k"].at[1, mine, :], before, 3, k_slot)
     k_in = expect(side["k"].at[:, mine, :], 3, k_slot)
-    u_in = [swap_all(["u0", "u1", "u2"], c) for c in range(CHUNKS)]
+    copies[0].wait()
+
+    @pl.when(gives)
+    def _():
+        k_src = pad["k"].at[pl.ds(pl.multiple_of(PAD + own, PAD), share), :]
+        put(k_src, side["k"].at[0, mine, :], after, 3, k_slot)
+        put(k_src, side["k"].at[1, mine, :], before, 3, k_slot)
+
+    for copy in copies[1:4]:
+        copy.wait()
+    u_in = [swap_all(["u0", "u1", "u2"], c) for c in each]
     put(inner("u2"), plane["xu"], next_device, 2, early)
-    arrive(k_in)
-    for s in range(2):
-        block = side["k"].at[s, mine, :]
-        for k in range(1, nt):
-            pltpu.make_async_remote_copy(
-                src_ref=block, dst_ref=block, send_sem=gsend.at[0], recv_sem=grecv.at[0],
-                device_id=t_peer(k), device_id_type=MESH,
-            ).start()
-    spread = side["k"].at[:, pl.ds(0, share * (nt - 1)), :]
-    shared = pltpu.make_async_remote_copy(
-        src_ref=spread, dst_ref=spread, send_sem=gsend.at[0], recv_sem=grecv.at[0],
-        device_id=after, device_id_type=MESH,
-    )
-    shared.wait_recv()
+    edge = jnp.zeros((PAD, cols), jnp.float32)
+    for name in PADDED:
+        pad[name][pl.ds(0, PAD), :] = edge
+        pad[name][pl.ds(PAD + rows, PAD), :] = edge
+    copies[4].wait()
+
+    def spread(region):
+        return pltpu.make_async_remote_copy(
+            src_ref=region, dst_ref=region, send_sem=gsend.at[0], recv_sem=grecv.at[0],
+            device_id=after, device_id_type=MESH,
+        )
+
+    @pl.when(gives)
+    def _():
+        arrive(k_in)
+        for s in range(2):
+            block = side["k"].at[s, mine, :]
+            for k in range(1, nt):
+                pltpu.make_async_remote_copy(
+                    src_ref=block, dst_ref=block, send_sem=gsend.at[0], recv_sem=grecv.at[0],
+                    device_id=t_peer(k), device_id_type=MESH,
+                ).start()
+        if givers > 1:
+            spread(side["k"].at[:, pl.ds(0, share * (givers - 1)), :]).wait_recv()
+
+    @pl.when(jnp.logical_not(gives))
+    def _():
+        spread(side["k"]).wait_recv()
 
     lane = lax.broadcasted_iota(jnp.int32, (BLOCK, cols), 1)
     first_lane, last_lane = lane == 0, lane == cols - 1
@@ -272,7 +289,7 @@
             device_id=after, device_id_type=MESH,
         )
 
-    bursts = [shared]
+    bursts = []
 
     def reduce_z(n, accs):
         rows_of = jnp.concatenate([lanes(acc) for acc in accs + [nothing] * (8 - len(accs))], axis=0)
@@ -304,8 +321,8 @@
         waits.wait_recv()
         return jnp.sum(xslots[0:ny, :], axis=0, keepdims=True)
 
-    def factors(sums, first, h):
-        s0, s1, s2, s3 = [sums[:, first + i:first + i + 1] for i in range(4)]
+    def factors(row, h):
+        s0, s1, s2, s3 = row, pltpu.roll(row, 127, 1), pltpu.roll(row, 126, 1), pltpu.roll(row, 125, 1)
         sigma = s1 / s0
         spread = jnp.maximum(s2 - s1 * sigma, 1e-30)
         bent = s3 - sigma * (s2 + s2) + sigma * sigma * s1
@@ -403,7 +420,7 @@
     take_b(each[:4])
     (y_wait,) = reduce_y(0, z_wait)
     take_b(each[4:])
-    c0, c1 = [whole(x) for x in factors(total_own(0, y_wait), 0, WIDTH[0])]
+    c0, c1 = [whole(x[:, 0:1]) for x in factors(total_own(0, y_wait), WIDTH[0])]
 
     def second_node(r, carry):
         s0, s1, s2 = carry
@@ -450,7 +467,7 @@
     (y_wait,) = reduce_y(1, z_wait)
     take_w(range(2, half))
     coarse = take_d(order[4:6], coarse)
-    e0, e1 = [whole(x) for x in factors(total_own(1, y_wait), 0, WIDTH[1])]
+    e0, e1 = [whole(x[:, 0:1]) for x in factors(total_own(1, y_wait), WIDTH[1])]
 
     def third_node(r, carry):
         s0, s1, s2 = carry
@@ -501,29 +518,30 @@
     expect(sides.at[pl.ds(1, len(SIDES) - 1)], 0, 0).wait_send()
     expect(planes.at[pl.ds(0, 2)], 1, 0).wait_send()
     expect(planes.at[pl.ds(0, 5)], 2, 0).wait_send()
-    k_in.wait_send()
+
+    @pl.when(gives)
+    def _():
+        k_in.wait_send()
+        spread(sides.at[pl.ds(0, 2), :, pl.ds(0, share * (nt - 1) // 2), :]).wait_send()
+
     for waits in bursts[:-2]:
         waits.wait_send()
-    g0, g1 = [whole(x) for x in factors(total_own(2, y_wait), 0, WIDTH[2])]
+    both = jnp.concatenate([total_own(2, y_wait), total_last(x_wait)], axis=0)
+    width = jnp.where(lax.broadcasted_iota(jnp.int32, (2, 128), 1) == 4, STEP, WIDTH[2])
+    f0, f1 = factors(both, width)
+    g0, g1 = whole(f0[0:1, 0:1]), whole(f1[0:1, 0:1])
+    passed = [x[1:2, q:q + 1] for q in (0, 4) for x in (f0, f1)]
+    p0, p1, q0, q1 = [whole(jnp.where(me_t == 0, 0.0, x)) for x in passed]
 
     def last_node(r, carry):
         at_pad = pl.ds(PAD + r, BLOCK)
-        move = g0 * plane["r3"][at(r), :] + g1 * pad["v3"][at_pad, :]
-        fine[2, at(r), :] = pad["u2"][at_pad, :] + move
-        return carry
-
-    sweep(0, rows, last_node, 0)
-    sums = total_last(x_wait)
-    passed = [jnp.where(me_t == 0, 0.0, x) for x in factors(sums, 0, WIDTH[2]) + factors(sums, 4, STEP)]
-    p0, p1, q0, q1 = [whole(x) for x in passed]
-
-    def next_slice(r, carry):
+        fine[2, at(r), :] = pad["u2"][at_pad, :] + (g0 * plane["r3"][at(r), :] + g1 * pad["v3"][at_pad, :])
         guess = plane["xu"][at(r), :]
         following[at(r), :] = guess + (p0 * plane["xr3"][at(r), :] + p1 * plane["xv3"][at(r), :])
         coarse_next[at(r), :] = guess + (q0 * plane["xrc"][at(r), :] + q1 * plane["xvc"][at(r), :])
         return carry
 
-    sweep(0, rows, next_slice, 0)
+    sweep(0, rows, last_node, 0)
     for waits in bursts[-2:]:
         waits.wait_send()
 
@@ -533,12 +551,16 @@
 
 
 def leave(fine, following, coarse, fine_hbm, following_hbm, coarse_hbm, sem):
-    copies = [
-        pltpu.make_async_copy(src, dst, sem.at[i])
-        for i, (src, dst) in enumerate(
-            [(fine, fine_hbm), (following, following_hbm), (coarse, coarse_hbm)]
-        )
-    ]
+    rows = following.shape[0] // 2
+    pairs = [(fine.at[m], fine_hbm.at[m]) for m in range(3)]
+    pairs += [(following, following_hbm), (coarse, coarse_hbm)]
+    copies = []
+    for src, dst in pairs:
+        for first in (0, rows):
+            part = pl.ds(first, rows)
+            copies.append(
+                pltpu.make_async_copy(src.at[part, :], dst.at[part, :], sem.at[len(copies)])
+            )
     for copy in copies:
         copy.start()
     for copy in copies:
@@ -587,7 +609,7 @@
         out_shape=(jax.ShapeDtypeStruct((3, rows, cols), jnp.float32), plane, plane),
         in_specs=[anywhere] * 3,
         out_specs=(anywhere,) * 3,
-        scratch_shapes=[pltpu.SemaphoreType.DMA((3,))],
+        scratch_shapes=[pltpu.SemaphoreType.DMA((10,))],
         compiler_params=pltpu.CompilerParams(vmem_limit_bytes=40 * 1024 * 1024),
     )(fine, following, coarse)
     return (

time: 139 us -> 138 us (level)
  no operation moved by 1% of the time
where the time goes in v6:
time: 138 us
  Pallas kernels  137 us (99%)
    pallas_call x1, Pallas kernels, on_device(): pl.pallas_call(functools.partial(kernel, dims), out_shape=(jax.ShapeDtype...  136 us

profile of v6, /device:TPU:1, one launch (start us, length us, event | category | flops | bytes accessed | tf_op | source)
XLA Modules:
  0.0 138.1 jit_solution(3483825718078305417)
XLA Ops:
  0.6 135.9 %shard_map.58 = (f32[3,512,256]{2,1,0:T(8,128)S(1)}, f32[512,256]{1,0:T(8,128)S(1)}, f32[512,256]{1,0:T(8,128)S(1)}) custom-call(f32[512,256]{1,0:T(8,128)} %bitcast.9, f32[3,512,256]{2,1,0:T(8,128)} %bitcast.8, f32[512,256]{1,0:T(8,128)} %bitcast.10), custom_call_target="tpu_custom_call" | custom-call | tf_op jit(solution)/shard_map/pallas_call | solution.py:583
  136.5 1.6 %shard_map.59 = (f32[3,512,256]{2,1,0:T(8,128)}, f32[512,256]{1,0:T(8,128)}, f32[512,256]{1,0:T(8,128)}) custom-call(f32[3,512,256]{2,1,0:T(8,128)S(1)} %get-tuple-element.9.fine, f32[512,256]{1,0:T(8,128)S(1)} %get-tuple-element.10.following, f32[512,256]{1,0:T(8,128)S(1)} %get-tuple-element.11.coarse), custom_call_target="tpu_custom_call" | custom-call | tf_op jit(solution)/shard_map/pallas_call | solution.py:607

commit v7 on v6

--- a/solution.py
+++ b/solution.py
@@ -43,7 +43,7 @@
 
 
 def kernel(dims, start_hbm, old_hbm, kappa_hbm, fine, following, coarse_next, padded, planes, sides,
-           tiles, ztiles, zslots, yslots, xslots, send, recv, gsend, grecv, local):
+           tiles, ztiles, zslots, yslots, xslots, send, recv, gsend, grecv, local, words):
     nt, ny, nz, rows, cols = dims
     chunk = rows // CHUNKS
     half = CHUNKS // 2
@@ -84,13 +84,26 @@
         copy.start()
     barrier = pltpu.get_barrier_semaphore()
     greeted = [after, before]
-    greeted += [z_peer(k) for k in range(1, nz)]
-    greeted += [y_peer(k) for k in range(1, ny)]
-    greeted += [t_peer(k) for k in range(1, nt)]
-    greeted += [y_peer(k, last_t) for k in range(ny)]
+    greeted += [z_peer(k) for k in (1, nz - 1)]
+    greeted += [y_peer(k) for k in (1, ny - 1)]
+    greeted += [t_peer(k) for k in (1, nt - 1)]
     for device in greeted:
         pl.semaphore_signal(barrier, inc=1, device_id=device, device_id_type=MESH)
     pl.semaphore_wait(barrier, len(greeted))
+
+    def ring_peers(k):
+        return [
+            peer(shift % size)
+            for peer, size in ((z_peer, nz), (y_peer, ny), (t_peer, nt))
+            for shift in (k, size - k)
+        ]
+
+    def tell(n, devices):
+        for device in devices:
+            pl.semaphore_signal(words.at[n], inc=1, device_id=device, device_id_type=MESH)
+
+    nearest, second = ring_peers(1), ring_peers(2)
+    third = [z_peer(2), z_peer(nz - 2), t_peer(1), t_peer(nt - 1)]
 
     taken = []
 
@@ -166,11 +179,16 @@
         copy.wait()
     u_in = [swap_all(["u0", "u1", "u2"], c) for c in each]
     put(inner("u2"), plane["xu"], next_device, 2, early)
+    tell(0, nearest)
     edge = jnp.zeros((PAD, cols), jnp.float32)
     for name in PADDED:
         pad[name][pl.ds(0, PAD), :] = edge
         pad[name][pl.ds(PAD + rows, PAD), :] = edge
     copies[4].wait()
+    pl.semaphore_wait(words.at[0], len(nearest))
+    tell(1, second)
+    pl.semaphore_wait(words.at[1], len(second))
+    tell(2, third)
 
     def spread(region):
         return pltpu.make_async_remote_copy(
@@ -195,6 +213,7 @@
     def _():
         spread(side["k"]).wait_recv()
 
+    pl.semaphore_wait(words.at[2], len(third))
     lane = lax.broadcasted_iota(jnp.int32, (BLOCK, cols), 1)
     first_lane, last_lane = lane == 0, lane == cols - 1
     zero = jnp.zeros((BLOCK, cols), jnp.float32)
@@ -599,6 +618,7 @@
             pltpu.SemaphoreType.DMA((10,)),
             pltpu.SemaphoreType.DMA((10,)),
             pltpu.SemaphoreType.DMA((5,)),
+            pltpu.SemaphoreType.REGULAR((3,)),
         ],
         compiler_params=pltpu.CompilerParams(
             collective_id=0, has_side_effects=True, vmem_limit_bytes=40 * 1024 * 1024

time: 138 us -> 136 us (0.986)
  Pallas kernels: 137 us -> 135 us
    pallas_call x1, Pallas kernels: 136 us -> 133 us  [on_device(): pl.pallas_call(functools.partial(kernel, dims), out_shape=(jax.ShapeDtype...]
where the time goes in v7:
time: 136 us; the launch traced here: 135 us
  Pallas kernels  135 us (99%)
    pallas_call x1, Pallas kernels, on_device(): pl.pallas_call(functools.partial(kernel, dims), out_shape=(jax.ShapeDtype...  133 us

profile of v7, /device:TPU:1, one launch (start us, length us, event | category | flops | bytes accessed | tf_op | source)
XLA Modules:
  0.0 135.5 jit_solution(4145504775565322510)
XLA Ops:
  0.6 133.2 %shard_map.58 = (f32[3,512,256]{2,1,0:T(8,128)S(1)}, f32[512,256]{1,0:T(8,128)S(1)}, f32[512,256]{1,0:T(8,128)S(1)}) custom-call(f32[512,256]{1,0:T(8,128)} %bitcast.9, f32[3,512,256]{2,1,0:T(8,128)} %bitcast.8, f32[512,256]{1,0:T(8,128)} %bitcast.10), custom_call_target="tpu_custom_call" | custom-call | tf_op jit(solution)/shard_map/pallas_call | solution.py:602
  133.9 1.6 %shard_map.59 = (f32[3,512,256]{2,1,0:T(8,128)}, f32[512,256]{1,0:T(8,128)}, f32[512,256]{1,0:T(8,128)}) custom-call(f32[3,512,256]{2,1,0:T(8,128)S(1)} %get-tuple-element.9.fine, f32[512,256]{1,0:T(8,128)S(1)} %get-tuple-element.10.following, f32[512,256]{1,0:T(8,128)S(1)} %get-tuple-element.11.coarse), custom_call_target="tpu_custom_call" | custom-call | tf_op jit(solution)/shard_map/pallas_call | solution.py:627

commit v8 on v7

--- a/solution.py
+++ b/solution.py
@@ -311,7 +311,9 @@
     bursts = []
 
     def reduce_z(n, accs):
-        rows_of = jnp.concatenate([lanes(acc) for acc in accs + [nothing] * (8 - len(accs))], axis=0)
+        rows_of = jnp.concatenate(
+            [acc if acc.shape[0] == 1 else lanes(acc) for acc in accs + [nothing] * (8 - len(accs))], axis=0
+        )
         sums = jnp.sum(rows_of, axis=1, keepdims=True)
         row = jnp.zeros((1, 128), jnp.float32)
         for q in range(len(accs)):
@@ -520,6 +522,8 @@
         arrive(vc_in[i])
         for c in (i, i + half):
             coarse3 = coarse3 + moments("vc", lambda s: plane["hvc"], c)
+    sums, coarse = [[lanes(acc) for acc in accs] for accs in (sums, coarse)]
+    coarse3 = lanes(coarse3)
     for i in range(half):
         arrive(v3_in[i])
         for c in (i, i + half):

time: 136 us -> 136 us (level)
  no operation moved by 1% of the time
where the time goes in v8:
time: 136 us; the launch traced here: 135 us
  Pallas kernels  135 us (99%)
    pallas_call x1, Pallas kernels, on_device(): pl.pallas_call(functools.partial(kernel, dims), out_shape=(jax.ShapeDtype...  133 us

profile of v8, /device:TPU:1, one launch (start us, length us, event | category | flops | bytes accessed | tf_op | source)
XLA Modules:
  0.0 135.5 jit_solution(16841190215855180563)
XLA Ops:
  0.6 133.2 %shard_map.58 = (f32[3,512,256]{2,1,0:T(8,128)S(1)}, f32[512,256]{1,0:T(8,128)S(1)}, f32[512,256]{1,0:T(8,128)S(1)}) custom-call(f32[512,256]{1,0:T(8,128)} %bitcast.9, f32[3,512,256]{2,1,0:T(8,128)} %bitcast.8, f32[512,256]{1,0:T(8,128)} %bitcast.10), custom_call_target="tpu_custom_call" | custom-call | tf_op jit(solution)/shard_map/pallas_call | solution.py:606
  133.9 1.6 %shard_map.59 = (f32[3,512,256]{2,1,0:T(8,128)}, f32[512,256]{1,0:T(8,128)}, f32[512,256]{1,0:T(8,128)}) custom-call(f32[3,512,256]{2,1,0:T(8,128)S(1)} %get-tuple-element.9.fine, f32[512,256]{1,0:T(8,128)S(1)} %get-tuple-element.10.following, f32[512,256]{1,0:T(8,128)S(1)} %get-tuple-element.11.coarse), custom_call_target="tpu_custom_call" | custom-call | tf_op jit(solution)/shard_map/pallas_call | solution.py:631
